TPU v7x, 128 devices: a whole 4x4x4 slice. The times are simulated.
128 devices in a mesh: res: 32 (over z, x, core), grp: 4 (over y).
Axes of the slice: x: 4, y: 4, z: 4, core: 2. Of those that a mesh axis runs over, the one named last changes fastest.
Arguments:
- right_side: float32 [3, 64, 64, 512], P(None, 'res', 'grp'), may hold values from -30 to 30
- accumulation: float32 [3, 3, 64, 64, 512], P(None, None, 'res', 'grp'), may hold values from -1 to 2, as said below
- transmissibility: float32 [6, 3, 3, 64, 64, 512], P(None, None, None, 'res', 'grp'), may hold values from -1 to 2, as said below
- completion: int32 [1024, 256], P(('res', 'grp')), may hold values from 0 to 16383, as said below
- live_count: int32 [1024], P(('res', 'grp')), may hold values from 64 to 256
- owner: int32 [1024, 1], P(('res', 'grp')), may hold values from 0 to 3; in each aligned block of 8 rows (0 to 7, 8 to 15, ...) at most 4 rows name the same one
- cell_to_well: float32 [1024, 3, 256], P(('res', 'grp')), may hold values from -3 to 3
- well_to_cell: float32 [1024, 3, 256], P(('res', 'grp')), may hold values from -3 to 3
- inverse: float32 [128, 4, 4, 256, 256], P(('res', 'grp')), may hold values from -1 to 2
Outputs:
- solution: float32 [3, 64, 64, 512], P(None, 'res', 'grp')
- residual: float32 [3, 64, 64, 512], P(None, 'res', 'grp')
Inputs may be any that keep to these rules, and one draw needn't show every extreme that they name: `completion`: cells may repeat. Among the 8 wells of one device at most 4 name the same owner. `accumulation`: diagonal entries positive. `transmissibility`: diagonal entries positive.
All inputs are finite; a program needn't handle non-finite values.
Results may differ from a plain program's by a relative error of at most 0.0003.
Values sent between devices are 32-bit elements; how exact they have to be, the bound alone decides.
A program may use at most 128 MiB of HBM per device.

v0:
```python
import jax
import jax.numpy as jnp
from jax import lax
from jax.sharding import Mesh
from jax.sharding import PartitionSpec as P

ITERS = 3
RES_GRP = ("res_0", "res_1", "res_2", "grp")
RES = ("res_0", "res_1", "res_2")


def extended(shard, sides, width):
    edges = {}
    for axis, dim in sides:
        devices, length = (lax.axis_size(axis), shard.shape[dim])
        up = [(i, (i + 1) % devices) for i in range(devices - 1)]
        last = lax.slice_in_dim(shard, length - width, length, axis=dim)
        leading = lax.slice_in_dim(shard, 0, width, axis=dim)
        edges[dim] = (
            lax.ppermute(last, axis, up),
            lax.ppermute(leading, axis, [(b, a) for a, b in up]),
        )
    done = []
    for _, dim in sides:
        low, high = edges[dim]
        around = [(width, width) if d in done else (0, 0) for d in range(shard.ndim)]
        shard = jnp.concatenate([jnp.pad(low, around), shard, jnp.pad(high, around)], axis=dim)
        done.append(dim)
    return shard


def over_axes(shard, axes):
    for axis in axes:
        shard = lax.psum(shard, axis)
    return shard


def neighbours(vector):
    padded = extended(vector, ((RES, 1), ("grp", 2)), 1)
    zpadded = jnp.pad(vector, ((0, 0), (0, 0), (0, 0), (1, 1)))
    return [
        padded[:, 2:, 1:-1, :],
        padded[:, :-2, 1:-1, :],
        padded[:, 1:-1, 2:, :],
        padded[:, 1:-1, :-2, :],
        zpadded[..., 2:],
        zpadded[..., :-2],
    ]


def stencil(vector, diag_total, transmissibility):
    beside_list = neighbours(vector)
    result = jnp.sum(diag_total * vector[None], axis=1)
    for face in range(6):
        result = result - jnp.sum(transmissibility[face] * beside_list[face][None], axis=1)
    return result


def body(
    right_side,
    accumulation,
    transmissibility,
    completion,
    live_count,
    owner,
    cell_to_well,
    well_to_cell,
    inverse,
):
    highest = lax.Precision.HIGHEST
    components, cells_x, cells_y, cells_z = right_side.shape
    blocks, segb = completion.shape
    capacity = inverse.shape[2]
    groups = lax.axis_size("grp")
    flat_index = completion.reshape(-1)
    open_mask = (jnp.arange(segb, dtype=jnp.int32)[None, :] < live_count[:, None]).astype(
        jnp.float32
    )
    owner_eq = (owner == jnp.arange(groups, dtype=jnp.int32)[None, :]).astype(jnp.int32)
    prior = jnp.cumsum(owner_eq, axis=0) - owner_eq
    slot_number = jnp.sum(prior * owner_eq, axis=1)
    target = owner[:, 0] * capacity + slot_number
    packing = (target[:, None] == jnp.arange(groups * capacity, dtype=jnp.int32)[None, :]).astype(
        jnp.float32
    )
    diag_total = accumulation
    for face in range(6):
        diag_total = diag_total + transmissibility[face]
    moved = lax.all_to_all(inverse[0], "grp", split_axis=0, concat_axis=0, tiled=True)
    block_inverse = jnp.einsum(
        "bq,qst->bst", packing, moved.reshape(groups * capacity, segb, segb), precision=highest
    )

    def solve_wells(coupled):
        return jnp.einsum("bst,bt->bs", block_inverse, coupled, precision=highest)

    def operator(vector):
        result = stencil(vector, diag_total, transmissibility)
        flat = vector.reshape(components, -1)
        picked = jnp.moveaxis(flat[:, flat_index].reshape(components, blocks, segb), 0, 1)
        coupled = jnp.sum(cell_to_well * picked, axis=1) * open_mask
        well_value = solve_wells(coupled)
        correction = well_to_cell * (well_value * open_mask)[:, None, :]
        correction = jnp.moveaxis(correction, 0, 1).reshape(components, -1)
        out_flat = result.reshape(components, -1).at[:, flat_index].add(-correction)
        return out_flat.reshape(vector.shape)

    solution = jnp.zeros_like(right_side)
    residual = right_side
    search = right_side
    rho = over_axes(jnp.sum(residual * residual), RES_GRP)
    for index in range(ITERS):
        image = operator(search)
        alpha = rho / over_axes(jnp.sum(right_side * image), RES_GRP)
        middle = residual - alpha * image
        second = operator(middle)
        inner, square, along_middle, along_second = (
            over_axes(jnp.sum(second * middle), RES_GRP),
            over_axes(jnp.sum(second * second), RES_GRP),
            over_axes(jnp.sum(right_side * middle), RES_GRP),
            over_axes(jnp.sum(right_side * second), RES_GRP),
        )
        omega = inner / square
        solution = solution + alpha * search + omega * middle
        residual = middle - omega * second
        rho_next = along_middle - omega * along_second
        if index + 1 < ITERS:
            search = residual + rho_next / rho * (alpha / omega) * (search - omega * image)
            rho = rho_next
    return (solution, residual)


def solution(mesh):
    finer = Mesh(
        mesh.devices.reshape(4, 4, 2, mesh.shape["grp"]), ("res_0", "res_1", "res_2", "grp")
    )
    in_specs = (
        P(None, RES, "grp", None),
        P(None, None, RES, "grp", None),
        P(None, None, None, RES, "grp", None),
        P(RES_GRP, None),
        P(RES_GRP),
        P(RES_GRP, None),
        P(RES_GRP, None, None),
        P(RES_GRP, None, None),
        P(RES_GRP, None, None, None, None),
    )
    out_specs = (P(None, RES, "grp", None), P(None, RES, "grp", None))
    return jax.shard_map(body, mesh=finer, in_specs=in_specs, out_specs=out_specs, check_vma=False)
```

profile of v0, /device:TPU:10, one launch (start us, length us, event | category | flops | bytes accessed | tf_op | source)
XLA Modules:
  0.0 719.7 jit_solution(10837892056741657385)
XLA Ops:
  27.1 11.0 %gather_fusion = f32[2048,3]{1,0:T(8,128)} fusion(f32[3,16384]{0,1:T(8,128)} %bitcast.284, s32[2048]{0:T(1024)S(1)} %broadcast_clamp_fusion), kind=kCustom, calls=%fused_computation | custom fusion | bytes 57344 | tf_op jit(solution)/shard_map/gather | solution.py:100
  74.2 17.7 %scatter_fusion = f32[3,16384]{0,1:T(8,128)} fusion(f32[3,16384]{0,1:T(8,128)} %bitcast.273, s32[2048]{0:T(1024)S(1)} %bitcast.299, f32[2048,3]{1,0:T(8,128)} %bitcast.291), kind=kCustom, calls=%fused_computation.6 | custom fusion | flops 6144 | bytes 81920 | tf_op jit(solution)/shard_map/scatter-add | solution.py:105
  99.4 12.4 %all-reduce.29 = (f32[]{:T(128)}, f32[]{:T(128)}) all-reduce(f32[]{:T(128)} %get-tuple-element.45, f32[]{:T(128)} %get-tuple-element.44), channel_id=1, replica_groups=mesh['res_0'=4,'res_1'=4,'res_2'=2,'grp'=4] {'res_0'}, use_global_device_ids=true, to_apply=%region_1.2 | all-reduce | flops 2 | bytes 16 | tf_op jit(solution)/shard_map/psum | solution.py:34
  111.9 11.0 %all-reduce.25 = (f32[]{:T(128)}, f32[]{:T(128)}) all-reduce(f32[]{:T(128)} %get-tuple-element.80, f32[]{:T(128)} %get-tuple-element.81), channel_id=1, replica_groups=mesh['res_0'=4,'res_1'=4,'res_2'=2,'grp'=4] {'res_1'}, use_global_device_ids=true, to_apply=%region_2.3 | all-reduce | flops 2 | bytes 16 | tf_op jit(solution)/shard_map/psum | solution.py:34
  126.0 8.7 %all-reduce.21 = (f32[]{:T(128)}, f32[]{:T(128)}) all-reduce(f32[]{:T(128)} %get-tuple-element.92, f32[]{:T(128)} %get-tuple-element.93), channel_id=1, replica_groups=mesh['res_0'=4,'res_1'=4,'res_2'=2,'grp'=4] {'grp'}, use_global_device_ids=true, to_apply=%region_4.5 | all-reduce | flops 2 | bytes 16 | tf_op jit(solution)/shard_map/psum | solution.py:34
  156.5 10.9 %gather_fusion.1 = f32[2048,3]{1,0:T(8,128)} fusion(f32[3,16384]{0,1:T(8,128)} %bitcast.280, s32[2048]{0:T(1024)S(1)} %broadcast_clamp_fusion), kind=kCustom, calls=%fused_computation.1 | custom fusion | bytes 57344 | tf_op jit(solution)/shard_map/gather | solution.py:100
  190.7 17.3 %scatter_fusion.1 = f32[3,16384]{0,1:T(8,128)} fusion(f32[3,16384]{0,1:T(8,128)} %bitcast.269, s32[2048]{0:T(1024)S(1)} %bitcast.300, f32[2048,3]{1,0:T(8,128)} %bitcast.288), kind=kCustom, calls=%fused_computation.7 | custom fusion | flops 6144 | bytes 81920 | tf_op jit(solution)/shard_map/scatter-add | solution.py:105
  220.9 8.4 %all-reduce.28 = (f32[]{:T(128)}, f32[]{:T(128)}, f32[]{:T(128)}, f32[]{:T(128)}) all-reduce(f32[]{:T(128)} %get-tuple-element.43, f32[]{:T(128)} %get-tuple-element.42, f32[]{:T(128)} %multiply_reduce_fusion.2, f32[]{:T(128)} %get-tuple-element.41), channel_id=1, replica_groups=mesh['res_0'=4,'res_1'=4,'res_2'=2,'grp'=4] {'res_0'}, use_global_device_ids=true, to_apply=%region_41.42 | all-reduce | flops 4 | bytes 32 | tf_op jit(solution)/shard_map/psum | solution.py:34
  229.4 11.5 %all-reduce.24 = (f32[]{:T(128)}, f32[]{:T(128)}, f32[]{:T(128)}, f32[]{:T(128)}) all-reduce(f32[]{:T(128)} %get-tuple-element.76, f32[]{:T(128)} %get-tuple-element.77, f32[]{:T(128)} %get-tuple-element.78, f32[]{:T(128)} %get-tuple-element.79), channel_id=1, replica_groups=mesh['res_0'=4,'res_1'=4,'res_2'=2,'grp'=4] {'res_1'}, use_global_device_ids=true, to_apply=%region_42.43 | all-reduce | flops 4 | bytes 32 | tf_op jit(solution)/shard_map/psum | solution.py:34
  278.4 10.9 %gather_fusion.2 = f32[2048,3]{1,0:T(8,128)} fusion(f32[3,16384]{0,1:T(8,128)} %bitcast.281, s32[2048]{0:T(1024)S(1)} %broadcast_clamp_fusion), kind=kCustom, calls=%fused_computation.2 | custom fusion | bytes 57344 | tf_op jit(solution)/shard_map/gather | solution.py:100
  312.8 17.3 %scatter_fusion.2 = f32[3,16384]{0,1:T(8,128)} fusion(f32[3,16384]{0,1:T(8,128)} %bitcast.275, s32[2048]{0:T(1024)S(1)} %bitcast.301, f32[2048,3]{1,0:T(8,128)} %bitcast.289), kind=kCustom, calls=%fused_computation.8 | custom fusion | flops 6144 | bytes 81920 | tf_op jit(solution)/shard_map/scatter-add | solution.py:105
  337.7 8.9 %psum.416 = f32[]{:T(128)} all-reduce(f32[]{:T(128)} %multiply_reduce_fusion.14), channel_id=1, replica_groups=mesh['res_0'=4,'res_1'=4,'res_2'=2,'grp'=4] {'res_0'}, use_global_device_ids=true, to_apply=%region_60.61 | all-reduce | flops 1 | bytes 8 | tf_op jit(solution)/shard_map/psum | solution.py:34
  346.6 11.5 %psum.417 = f32[]{:T(128)} all-reduce(f32[]{:T(128)} %psum.416), channel_id=1, replica_groups=mesh['res_0'=4,'res_1'=4,'res_2'=2,'grp'=4] {'res_1'}, use_global_device_ids=true, to_apply=%region_61.62 | all-reduce | flops 1 | bytes 8 | tf_op jit(solution)/shard_map/psum | solution.py:34
  390.4 10.9 %gather_fusion.3 = f32[2048,3]{1,0:T(8,128)} fusion(f32[3,16384]{0,1:T(8,128)} %bitcast.282, s32[2048]{0:T(1024)S(1)} %broadcast_clamp_fusion), kind=kCustom, calls=%fused_computation.3 | custom fusion | bytes 57344 | tf_op jit(solution)/shard_map/gather | solution.py:100
  424.7 17.3 %scatter_fusion.3 = f32[3,16384]{0,1:T(8,128)} fusion(f32[3,16384]{0,1:T(8,128)} %bitcast.271, s32[2048]{0:T(1024)S(1)} %bitcast.302, f32[2048,3]{1,0:T(8,128)} %bitcast.290), kind=kCustom, calls=%fused_computation.9 | custom fusion | flops 6144 | bytes 81920 | tf_op jit(solution)/shard_map/scatter-add | solution.py:105
  454.9 8.4 %all-reduce.27 = (f32[]{:T(128)}, f32[]{:T(128)}, f32[]{:T(128)}, f32[]{:T(128)}) all-reduce(f32[]{:T(128)} %get-tuple-element.40, f32[]{:T(128)} %get-tuple-element.39, f32[]{:T(128)} %multiply_reduce_fusion.1, f32[]{:T(128)} %get-tuple-element.38), channel_id=1, replica_groups=mesh['res_0'=4,'res_1'=4,'res_2'=2,'grp'=4] {'res_0'}, use_global_device_ids=true, to_apply=%region_84.85 | all-reduce | flops 4 | bytes 32 | tf_op jit(solution)/shard_map/psum | solution.py:34
  463.3 11.2 %all-reduce.23 = (f32[]{:T(128)}, f32[]{:T(128)}, f32[]{:T(128)}, f32[]{:T(128)}) all-reduce(f32[]{:T(128)} %get-tuple-element.72, f32[]{:T(128)} %get-tuple-element.73, f32[]{:T(128)} %get-tuple-element.74, f32[]{:T(128)} %get-tuple-element.75), channel_id=1, replica_groups=mesh['res_0'=4,'res_1'=4,'res_2'=2,'grp'=4] {'res_1'}, use_global_device_ids=true, to_apply=%region_85.86 | all-reduce | flops 4 | bytes 32 | tf_op jit(solution)/shard_map/psum | solution.py:34
  510.9 10.9 %gather_fusion.4 = f32[2048,3]{1,0:T(8,128)} fusion(f32[3,16384]{0,1:T(8,128)} %bitcast.283, s32[2048]{0:T(1024)S(1)} %broadcast_clamp_fusion), kind=kCustom, calls=%fused_computation.4 | custom fusion | bytes 57344 | tf_op jit(solution)/shard_map/gather | solution.py:100
  545.1 17.3 %scatter_fusion.4 = f32[3,16384]{0,1:T(8,128)} fusion(f32[3,16384]{0,1:T(8,128)} %bitcast.277, s32[2048]{0:T(1024)S(1)} %bitcast.303, f32[2048,3]{1,0:T(8,128)} %bitcast.286), kind=kCustom, calls=%fused_computation.10 | custom fusion | flops 6144 | bytes 81920 | tf_op jit(solution)/shard_map/scatter-add | solution.py:105
  578.4 11.9 %psum.437 = f32[]{:T(128)} all-reduce(f32[]{:T(128)} %psum.436), channel_id=1, replica_groups=mesh['res_0'=4,'res_1'=4,'res_2'=2,'grp'=4] {'res_1'}, use_global_device_ids=true, to_apply=%region_104.105 | all-reduce | flops 1 | bytes 8 | tf_op jit(solution)/shard_map/psum | solution.py:34
  622.4 10.9 %gather_fusion.5 = f32[2048,3]{1,0:T(8,128)} fusion(f32[3,16384]{0,1:T(8,128)} %bitcast.279, s32[2048]{0:T(1024)S(1)} %broadcast_clamp_fusion), kind=kCustom, calls=%fused_computation.5 | custom fusion | bytes 57344 | tf_op jit(solution)/shard_map/gather | solution.py:100
  655.0 17.3 %scatter_fusion.5 = f32[3,16384]{0,1:T(8,128)} fusion(f32[3,16384]{0,1:T(8,128)} %bitcast.267, s32[2048]{0:T(1024)S(1)} %bitcast.304, f32[2048,3]{1,0:T(8,128)} %bitcast.287), kind=kCustom, calls=%fused_computation.11 | custom fusion | flops 6144 | bytes 81920 | tf_op jit(solution)/shard_map/scatter-add | solution.py:105
  691.8 11.0 %all-reduce.22 = (f32[]{:T(128)}, f32[]{:T(128)}) all-reduce(f32[]{:T(128)} %get-tuple-element.70, f32[]{:T(128)} %get-tuple-element.71), channel_id=1, replica_groups=mesh['res_0'=4,'res_1'=4,'res_2'=2,'grp'=4] {'res_1'}, use_global_device_ids=true, to_apply=%region_118.119 | all-reduce | flops 2 | bytes 16 | tf_op jit(solution)/shard_map/psum | solution.py:34
  705.8 11.0 %all-reduce.18 = (f32[]{:T(128)}, f32[]{:T(128)}) all-reduce(f32[]{:T(128)} %get-tuple-element.82, f32[]{:T(128)} %get-tuple-element.83), channel_id=1, replica_groups=mesh['res_0'=4,'res_1'=4,'res_2'=2,'grp'=4] {'grp'}, use_global_device_ids=true, to_apply=%region_120.121 | all-reduce | flops 2 | bytes 16 | tf_op jit(solution)/shard_map/psum | solution.py:34
  (218 shorter events, 407.8 us)
Async XLA Ops:
  0.7 60.2 %all-to-all-start = ((f32[4,4,256,256]{3,2,1,0:T(8,128)}), f32[4,4,256,256]{3,2,1,0:T(8,128)}, u32[]{:S(2)}, u32[]{:S(2)}) async-start(f32[4,4,256,256]{3,2,1,0:T(8,128)} %bitcast.285), calls=%async_computation | async-start | bytes 8388608 | tf_op jit(solution)/shard_map/all_to_all | solution.py:89
  7.8 45.1 %collective-permute-start.3 = (f32[3,2,1,512]{3,2,1,0:T(1,128)}, f32[3,2,1,512]{3,2,1,0:T(1,128)}, u32[]{:S(2)}, u32[]{:S(2)}) collective-permute-start(f32[3,2,1,512]{3,2,1,0:T(1,128)} %get-tuple-element.171), channel_id=1, source_target_pairs={{0,1},{1,2},{2,3},{4,5},{5,6},{6,7},{8,9},{9,10},{10,11},{12,13},{... | collective-permute-start | bytes 36872 | tf_op jit(solution)/shard_map/ppermute | solution.py:20
  11.2 41.8 %collective-permute-start.2 = (f32[3,2,1,512]{3,2,1,0:T(1,128)}, f32[3,2,1,512]{3,2,1,0:T(1,128)}, u32[]{:S(2)}, u32[]{:S(2)}) collective-permute-start(f32[3,2,1,512]{3,2,1,0:T(1,128)} %get-tuple-element.172), channel_id=1, source_target_pairs={{1,0},{2,1},{3,2},{5,4},{6,5},{7,6},{9,8},{10,9},{11,10},{13,12},{... | collective-permute-start | bytes 36872 | tf_op jit(solution)/shard_map/ppermute | solution.py:21
  15.9 33.6 %collective-permute-start.1 = (f32[3,1,16,512]{3,2,1,0:T(8,128)}, f32[3,1,16,512]{3,2,1,0:T(8,128)}, u32[]{:S(2)}, u32[]{:S(2)}) collective-permute-start(f32[3,1,16,512]{3,2,1,0:T(8,128)} %get-tuple-element.173), channel_id=1, source_target_pairs={{0,4},{4,8},{8,12},{12,16},{16,20},{20,24},{24,28},{28,32},{32,36}... | collective-permute-start | bytes 294920 | tf_op jit(solution)/shard_map/ppermute | solution.py:20
  17.8 32.6 %collective-permute-start = (f32[3,1,16,512]{3,2,1,0:T(8,128)}, f32[3,1,16,512]{3,2,1,0:T(8,128)}, u32[]{:S(2)}, u32[]{:S(2)}) collective-permute-start(f32[3,1,16,512]{3,2,1,0:T(8,128)} %get-tuple-element.174), channel_id=1, source_target_pairs={{4,0},{8,4},{12,8},{16,12},{20,16},{24,20},{28,24},{32,28},{36,32}... | collective-permute-start | bytes 294920 | tf_op jit(solution)/shard_map/ppermute | solution.py:21
  144.2 36.9 %collective-permute-start.7 = (f32[3,2,1,512]{3,2,1,0:T(1,128)}, f32[3,2,1,512]{3,2,1,0:T(1,128)}, u32[]{:S(2)}, u32[]{:S(2)}) collective-permute-start(f32[3,2,1,512]{3,2,1,0:T(1,128)} %get-tuple-element.162), channel_id=1, source_target_pairs={{0,1},{1,2},{2,3},{4,5},{5,6},{6,7},{8,9},{9,10},{10,11},{12,13},{... | collective-permute-start | bytes 36872 | tf_op jit(solution)/shard_map/ppermute | solution.py:20
  147.8 33.2 %collective-permute-start.6 = (f32[3,2,1,512]{3,2,1,0:T(1,128)}, f32[3,2,1,512]{3,2,1,0:T(1,128)}, u32[]{:S(2)}, u32[]{:S(2)}) collective-permute-start(f32[3,2,1,512]{3,2,1,0:T(1,128)} %get-tuple-element.163), channel_id=1, source_target_pairs={{1,0},{2,1},{3,2},{5,4},{6,5},{7,6},{9,8},{10,9},{11,10},{13,12},{... | collective-permute-start | bytes 36872 | tf_op jit(solution)/shard_map/ppermute | solution.py:21
  150.9 30.1 %collective-permute-start.5 = (f32[3,1,16,512]{3,2,1,0:T(8,128)}, f32[3,1,16,512]{3,2,1,0:T(8,128)}, u32[]{:S(2)}, u32[]{:S(2)}) collective-permute-start(f32[3,1,16,512]{3,2,1,0:T(8,128)} %get-tuple-element.164), channel_id=1, source_target_pairs={{0,4},{4,8},{8,12},{12,16},{16,20},{20,24},{24,28},{28,32},{32,36}... | collective-permute-start | bytes 294920 | tf_op jit(solution)/shard_map/ppermute | solution.py:20
  266.2 36.7 %collective-permute-start.11 = (f32[3,2,1,512]{3,2,1,0:T(1,128)}, f32[3,2,1,512]{3,2,1,0:T(1,128)}, u32[]{:S(2)}, u32[]{:S(2)}) collective-permute-start(f32[3,2,1,512]{3,2,1,0:T(1,128)} %get-tuple-element.152), channel_id=1, source_target_pairs={{0,1},{1,2},{2,3},{4,5},{5,6},{6,7},{8,9},{9,10},{10,11},{12,13},{... | collective-permute-start | bytes 36872 | tf_op jit(solution)/shard_map/ppermute | solution.py:20
  269.3 33.7 %collective-permute-start.10 = (f32[3,2,1,512]{3,2,1,0:T(1,128)}, f32[3,2,1,512]{3,2,1,0:T(1,128)}, u32[]{:S(2)}, u32[]{:S(2)}) collective-permute-start(f32[3,2,1,512]{3,2,1,0:T(1,128)} %get-tuple-element.153), channel_id=1, source_target_pairs={{1,0},{2,1},{3,2},{5,4},{6,5},{7,6},{9,8},{10,9},{11,10},{13,12},{... | collective-permute-start | bytes 36872 | tf_op jit(solution)/shard_map/ppermute | solution.py:21
  272.7 30.3 %collective-permute-start.9 = (f32[3,1,16,512]{3,2,1,0:T(8,128)}, f32[3,1,16,512]{3,2,1,0:T(8,128)}, u32[]{:S(2)}, u32[]{:S(2)}) collective-permute-start(f32[3,1,16,512]{3,2,1,0:T(8,128)} %get-tuple-element.154), channel_id=1, source_target_pairs={{0,4},{4,8},{8,12},{12,16},{16,20},{20,24},{24,28},{28,32},{32,36}... | collective-permute-start | bytes 294920 | tf_op jit(solution)/shard_map/ppermute | solution.py:20
  274.6 28.4 %collective-permute-start.8 = (f32[3,1,16,512]{3,2,1,0:T(8,128)}, f32[3,1,16,512]{3,2,1,0:T(8,128)}, u32[]{:S(2)}, u32[]{:S(2)}) collective-permute-start(f32[3,1,16,512]{3,2,1,0:T(8,128)} %get-tuple-element.155), channel_id=1, source_target_pairs={{4,0},{8,4},{12,8},{16,12},{20,16},{24,20},{28,24},{32,28},{36,32}... | collective-permute-start | bytes 294920 | tf_op jit(solution)/shard_map/ppermute | solution.py:21
  378.2 36.8 %collective-permute-start.15 = (f32[3,2,1,512]{3,2,1,0:T(1,128)}, f32[3,2,1,512]{3,2,1,0:T(1,128)}, u32[]{:S(2)}, u32[]{:S(2)}) collective-permute-start(f32[3,2,1,512]{3,2,1,0:T(1,128)} %get-tuple-element.142), channel_id=1, source_target_pairs={{0,1},{1,2},{2,3},{4,5},{5,6},{6,7},{8,9},{9,10},{10,11},{12,13},{... | collective-permute-start | bytes 36872 | tf_op jit(solution)/shard_map/ppermute | solution.py:20
  381.2 33.8 %collective-permute-start.14 = (f32[3,2,1,512]{3,2,1,0:T(1,128)}, f32[3,2,1,512]{3,2,1,0:T(1,128)}, u32[]{:S(2)}, u32[]{:S(2)}) collective-permute-start(f32[3,2,1,512]{3,2,1,0:T(1,128)} %get-tuple-element.143), channel_id=1, source_target_pairs={{1,0},{2,1},{3,2},{5,4},{6,5},{7,6},{9,8},{10,9},{11,10},{13,12},{... | collective-permute-start | bytes 36872 | tf_op jit(solution)/shard_map/ppermute | solution.py:21
  384.6 30.3 %collective-permute-start.13 = (f32[3,1,16,512]{3,2,1,0:T(8,128)}, f32[3,1,16,512]{3,2,1,0:T(8,128)}, u32[]{:S(2)}, u32[]{:S(2)}) collective-permute-start(f32[3,1,16,512]{3,2,1,0:T(8,128)} %get-tuple-element.144), channel_id=1, source_target_pairs={{0,4},{4,8},{8,12},{12,16},{16,20},{20,24},{24,28},{28,32},{32,36}... | collective-permute-start | bytes 294920 | tf_op jit(solution)/shard_map/ppermute | solution.py:20
  386.5 28.4 %collective-permute-start.12 = (f32[3,1,16,512]{3,2,1,0:T(8,128)}, f32[3,1,16,512]{3,2,1,0:T(8,128)}, u32[]{:S(2)}, u32[]{:S(2)}) collective-permute-start(f32[3,1,16,512]{3,2,1,0:T(8,128)} %get-tuple-element.145), channel_id=1, source_target_pairs={{4,0},{8,4},{12,8},{16,12},{20,16},{24,20},{28,24},{32,28},{36,32}... | collective-permute-start | bytes 294920 | tf_op jit(solution)/shard_map/ppermute | solution.py:21
  498.7 36.8 %collective-permute-start.19 = (f32[3,2,1,512]{3,2,1,0:T(1,128)}, f32[3,2,1,512]{3,2,1,0:T(1,128)}, u32[]{:S(2)}, u32[]{:S(2)}) collective-permute-start(f32[3,2,1,512]{3,2,1,0:T(1,128)} %get-tuple-element.132), channel_id=1, source_target_pairs={{0,1},{1,2},{2,3},{4,5},{5,6},{6,7},{8,9},{9,10},{10,11},{12,13},{... | collective-permute-start | bytes 36872 | tf_op jit(solution)/shard_map/ppermute | solution.py:20
  501.6 33.8 %collective-permute-start.18 = (f32[3,2,1,512]{3,2,1,0:T(1,128)}, f32[3,2,1,512]{3,2,1,0:T(1,128)}, u32[]{:S(2)}, u32[]{:S(2)}) collective-permute-start(f32[3,2,1,512]{3,2,1,0:T(1,128)} %get-tuple-element.133), channel_id=1, source_target_pairs={{1,0},{2,1},{3,2},{5,4},{6,5},{7,6},{9,8},{10,9},{11,10},{13,12},{... | collective-permute-start | bytes 36872 | tf_op jit(solution)/shard_map/ppermute | solution.py:21
  505.1 30.4 %collective-permute-start.17 = (f32[3,1,16,512]{3,2,1,0:T(8,128)}, f32[3,1,16,512]{3,2,1,0:T(8,128)}, u32[]{:S(2)}, u32[]{:S(2)}) collective-permute-start(f32[3,1,16,512]{3,2,1,0:T(8,128)} %get-tuple-element.134), channel_id=1, source_target_pairs={{0,4},{4,8},{8,12},{12,16},{16,20},{20,24},{24,28},{28,32},{32,36}... | collective-permute-start | bytes 294920 | tf_op jit(solution)/shard_map/ppermute | solution.py:20
  507.0 28.5 %collective-permute-start.16 = (f32[3,1,16,512]{3,2,1,0:T(8,128)}, f32[3,1,16,512]{3,2,1,0:T(8,128)}, u32[]{:S(2)}, u32[]{:S(2)}) collective-permute-start(f32[3,1,16,512]{3,2,1,0:T(8,128)} %get-tuple-element.135), channel_id=1, source_target_pairs={{4,0},{8,4},{12,8},{16,12},{20,16},{24,20},{28,24},{32,28},{36,32}... | collective-permute-start | bytes 294920 | tf_op jit(solution)/shard_map/ppermute | solution.py:21
  610.4 36.6 %collective-permute-start.22 = (f32[3,2,1,512]{3,2,1,0:T(1,128)}, f32[3,2,1,512]{3,2,1,0:T(1,128)}, u32[]{:S(2)}, u32[]{:S(2)}) collective-permute-start(f32[3,2,1,512]{3,2,1,0:T(1,128)} %get-tuple-element.122), channel_id=1, source_target_pairs={{1,0},{2,1},{3,2},{5,4},{6,5},{7,6},{9,8},{10,9},{11,10},{13,12},{... | collective-permute-start | bytes 36872 | tf_op jit(solution)/shard_map/ppermute | solution.py:21
  614.6 32.4 %collective-permute-start.23 = (f32[3,2,1,512]{3,2,1,0:T(1,128)}, f32[3,2,1,512]{3,2,1,0:T(1,128)}, u32[]{:S(2)}, u32[]{:S(2)}) collective-permute-start(f32[3,2,1,512]{3,2,1,0:T(1,128)} %get-tuple-element.123), channel_id=1, source_target_pairs={{0,1},{1,2},{2,3},{4,5},{5,6},{6,7},{8,9},{9,10},{10,11},{12,13},{... | collective-permute-start | bytes 36872 | tf_op jit(solution)/shard_map/ppermute | solution.py:20
  616.5 30.5 %collective-permute-start.21 = (f32[3,1,16,512]{3,2,1,0:T(8,128)}, f32[3,1,16,512]{3,2,1,0:T(8,128)}, u32[]{:S(2)}, u32[]{:S(2)}) collective-permute-start(f32[3,1,16,512]{3,2,1,0:T(8,128)} %get-tuple-element.124), channel_id=1, source_target_pairs={{0,4},{4,8},{8,12},{12,16},{16,20},{20,24},{24,28},{28,32},{32,36}... | collective-permute-start | bytes 294920 | tf_op jit(solution)/shard_map/ppermute | solution.py:20
  618.5 28.6 %collective-permute-start.20 = (f32[3,1,16,512]{3,2,1,0:T(8,128)}, f32[3,1,16,512]{3,2,1,0:T(8,128)}, u32[]{:S(2)}, u32[]{:S(2)}) collective-permute-start(f32[3,1,16,512]{3,2,1,0:T(8,128)} %get-tuple-element.125), channel_id=1, source_target_pairs={{4,0},{8,4},{12,8},{16,12},{20,16},{24,20},{28,24},{32,28},{36,32}... | collective-permute-start | bytes 294920 | tf_op jit(solution)/shard_map/ppermute | solution.py:21
  (18 other events, 411.7 us)
where the time goes:
time: 734 us; the launch traced here: 720 us
  local copies, waits for them, and re-layouts  205 us (28%)
  other arithmetic  197 us (27%)
  blocking collectives  194 us (26%)
  starting transfers between devices  78.4 us (11%)
  matrix products  28.8 us (4%)
  between operations  16.1 us (2%)
    psum x24, blocking collectives, over_axes(): shard = lax.psum(shard, axis)  194 us
    scatter-add x6, other arithmetic, operator(): out_flat = result.reshape(components, -1).at[:, flat_index].add(-correction)  104 us
    gather x6, local copies, waits for them, and re-layouts, operator(): flat[:, flat_index].reshape(components, blocks, segb)  65.7 us
    ppermute x12, starting transfers between devices, extended(): lax.ppermute(leading, axis, [(b, a) for a, b in up])  43.3 us
    reshape x6, local copies, waits for them, and re-layouts, operator(): return out_flat.reshape(vector.shape)  34.5 us
    sub x6, local copies, waits for them, and re-layouts, stencil(): result - jnp.sum(transmissibility[face] * beside_list[face][None], axis=1)  32.8 us
    ppermute x12, starting transfers between devices, extended(): lax.ppermute(last, axis, up)  29.4 us
    dot_general x6, matrix products, solve_wells(): return jnp.einsum('bst,bt->bs', block_inverse, coupled, precision=highest)  22.8 us
  transfers between devices with their start and end apart: 25, of which 0 were waited for; matrix products, arithmetic and copies ran while one was open for 23% of the time, Pallas kernels for 0%

commit v1 on v0

v1 whole, which is shorter than its diff:
```python
import functools

import jax
import jax.numpy as jnp
from jax import lax
from jax.experimental import pallas as pl
from jax.experimental.pallas import tpu as pltpu
from jax.sharding import PartitionSpec as P

ITERS = 3
RES_GRP = ("res", "grp")
MESH = pl.DeviceIdType.MESH
F32, BF16 = jnp.float32, jnp.bfloat16
R0, R, W, T, PP, S, Z, V, X, Q, Y = range(11)


def kernel(
    n_res,
    n_grp,
    live_ref,
    owner_ref,
    rhs_hbm,
    acc_hbm,
    trans_hbm,
    comp_hbm,
    c2w_hbm,
    w2c_hbm,
    inv_hbm,
    x_out,
    r_out,
    fld,
    diag,
    trans,
    inv,
    comp,
    c2w,
    w2c,
    picks,
    spread,
    hot,
    grid_of,
    lhs,
    xs,
    hx,
    hy,
    ysend,
    csend,
    crecv,
    vsend,
    vrecv,
    rsend,
    rrecv,
    scal,
    in_sem,
    hx_ss,
    hx_rs,
    hy_ss,
    hy_rs,
    c_ss,
    c_rs,
    v_ss,
    v_rs,
    r_ss,
    r_rs,
    out_sem,
):
    n_dev = n_res * n_grp
    r, g = lax.axis_index("res"), lax.axis_index("grp")
    me = r * n_grp + g

    def load(i, src, dst):
        return pltpu.make_async_copy(src, dst, in_sem.at[i])

    loads = [
        load(0, comp_hbm, comp),
        load(1, c2w_hbm, c2w),
        load(2, w2c_hbm, w2c),
        load(3, rhs_hbm, fld.at[R0]),
        load(4, acc_hbm, diag),
    ]
    loads += [load(5 + f, trans_hbm.at[f], trans.at[f]) for f in range(6)]
    loads += [load(11 + h, inv_hbm.at[0, h], inv.at[h]) for h in range(4)]
    for copy in loads:
        copy.start()

    hx[...] = jnp.zeros_like(hx)
    hy[...] = jnp.zeros_like(hy)

    barrier = pltpu.get_barrier_semaphore()

    def peer(k):
        other = lax.rem(me + k, n_dev)
        return (lax.div(other, n_grp), lax.rem(other, n_grp))

    def greet(k, carry):
        pl.semaphore_signal(barrier, inc=1, device_id=peer(k), device_id_type=MESH)
        return carry

    lax.fori_loop(1, n_dev, greet, 0)

    for field in (PP, S, Z, V, X):
        fld[field] = jnp.zeros((3, 2, 16, 512), F32)
    scal[...] = jnp.ones_like(scal)
    csend[...] = jnp.zeros_like(csend)
    ysend[...] = jnp.zeros_like(ysend)

    owners = [owner_ref[b, 0] for b in range(8)]
    target = []
    for b in range(8):
        slot = jnp.int32(0)
        for a in range(b):
            slot = slot + jnp.where(owners[a] == owners[b], 1, 0).astype(jnp.int32)
        target.append(lax.rem(owners[b] - g + n_grp, n_grp) * 8 + slot)

    for copy in loads[:3]:
        copy.wait()
    seg = lax.broadcasted_iota(jnp.int32, (1, 256), 1)
    for b in range(8):
        opened = seg < live_ref[b]
        c2w[b] = jnp.where(opened, c2w[b], 0.0)
        w2c[b] = jnp.where(opened, w2c[b], 0.0)
        cell = comp[b : b + 1, :]
        low = cell & 255
        half = (cell >> 8) & 1
        high = cell >> 9
        one = jnp.where(lax.broadcasted_iota(jnp.int32, (256, 256), 0) == low, 1.0, 0.0).astype(F32)
        picks[b] = one.astype(BF16)
        spread[b * 256 : (b + 1) * 256, :] = jnp.transpose(one).astype(BF16)
        rows = lax.broadcasted_iota(jnp.int32, (32, 256), 0)
        for zh in range(2):
            here = (rows == high) & (half == zh)
            hot[b, zh] = jnp.where(here, 1.0, 0.0).astype(BF16)
            for i in range(3):
                grid_of[b, zh * 96 + i * 32 : zh * 96 + (i + 1) * 32, :] = jnp.where(
                    here, c2w[b, i : i + 1, :], 0.0
                )

    for copy in loads[3:11]:
        copy.wait()
    for x in range(2):
        for i in range(3):
            for j in range(3):
                total = diag[i, j, x]
                for f in range(6):
                    total = total + trans[f, i, j, x]
                diag[i, j, x] = total
    for i in range(3):
        fld[R, i] = fld[R0, i]
    for copy in loads[11:]:
        copy.wait()

    pl.semaphore_wait(barrier, n_dev - 1)

    def remote(src, dst, ss, rs, device):
        return pltpu.make_async_remote_copy(
            src_ref=src, dst_ref=dst, send_sem=ss, recv_sem=rs, device_id=device, device_id_type=MESH
        )

    lane512 = lax.broadcasted_iota(jnp.int32, (8, 512), 1)
    row8 = lax.broadcasted_iota(jnp.int32, (8, 512), 0)
    iota32 = lax.broadcasted_iota(jnp.int32, (32, 256), 0)
    lane = lax.broadcasted_iota(jnp.int32, (1, 128), 1)

    def spmv(src, dst, par):
        x_up = remote(fld.at[src, :, 1], hx.at[par, 0], hx_ss.at[0], hx_rs.at[par, 0], (r + 1, g))
        x_dn = remote(fld.at[src, :, 0], hx.at[par, 1], hx_ss.at[1], hx_rs.at[par, 1], (r - 1, g))
        y_up = remote(ysend.at[0], hy.at[par, 0], hy_ss.at[0], hy_rs.at[par, 0], (r, g + 1))
        y_dn = remote(ysend.at[1], hy.at[par, 1], hy_ss.at[1], hy_rs.at[par, 1], (r, g - 1))
        pl.when(r < n_res - 1)(x_up.start)
        pl.when(r > 0)(x_dn.start)
        for j in range(3):
            for x in range(2):
                at = j * 2 + x
                ysend[0, at : at + 1, :] = fld[src, j, x, 15:16, :]
                ysend[1, at : at + 1, :] = fld[src, j, x, 0:1, :]
        pl.when(g < n_grp - 1)(y_up.start)
        pl.when(g > 0)(y_dn.start)

        for zh in range(2):
            v = fld[src, :, :, :, zh * 256 : (zh + 1) * 256].reshape(96, 256)
            top = v.astype(BF16)
            lhs[zh * 96 : (zh + 1) * 96, :] = top
            lhs[192 + zh * 96 : 192 + (zh + 1) * 96, :] = (v - top.astype(F32)).astype(BF16)
        out = jnp.zeros((32, 256), F32)
        for b in range(8):
            got = jnp.dot(lhs[...], picks[b], preferred_element_type=F32)
            row = jnp.sum((got[:192] + got[192:]) * grid_of[b], axis=0, keepdims=True)
            out = jnp.where(iota32 == target[b], row, out)
        csend[...] = out.reshape(4, 8, 256)
        c_copies = {}
        for d in (2, 1, 3):
            to = (r, lax.rem(g + d, n_grp))
            c_copies[d] = remote(csend.at[d], crecv.at[par, 4 - d], c_ss.at[d], c_rs.at[par, 4 - d], to)
            c_copies[d].start()

        for x in range(2):
            for yt in range(2):
                ys = slice(yt * 8, yt * 8 + 8)
                sums = [None] * 3
                for j in range(3):
                    v = fld[src, j, x, ys, :]
                    zp = jnp.where(lane512 == 511, 0.0, pltpu.roll(v, 511, 1))
                    zm = jnp.where(lane512 == 0, 0.0, pltpu.roll(v, 1, 1))
                    if yt == 0:
                        yp = fld[src, j, x, 1:9, :]
                        ym = jnp.where(row8 == 0, 0.0, pltpu.roll(v, 1, 0))
                    else:
                        yp = jnp.where(row8 == 7, 0.0, pltpu.roll(v, 7, 0))
                        ym = fld[src, j, x, 7:15, :]
                    xn = fld[src, j, 1 - x, ys, :]
                    for i in range(3):
                        part = diag[i, j, x, ys, :] * v
                        part = part - trans[x, i, j, x, ys, :] * xn
                        part = part - trans[2, i, j, x, ys, :] * yp
                        part = part - trans[3, i, j, x, ys, :] * ym
                        part = part - trans[4, i, j, x, ys, :] * zp
                        part = part - trans[5, i, j, x, ys, :] * zm
                        sums[i] = part if sums[i] is None else sums[i] + part
                for i in range(3):
                    fld[dst, i, x, ys, :] = sums[i]

        lane128 = lax.broadcasted_iota(jnp.int32, (256, 128), 1)
        v_copies = {}
        for d in (0, 1, 3, 2):
            home = lax.rem(g + d, n_grp)
            if d == 0:
                c8 = csend[0]
            else:
                remote(csend.at[d], crecv.at[par, d], c_ss.at[d], c_rs.at[par, d], (r, home)).wait_recv()
                c8 = crecv[par, d]
            columns = jnp.zeros((256, 128), F32)
            for k in range(4):
                column = jnp.sum(inv[home, k] * c8[k : k + 1, :], axis=1, keepdims=True)
                columns = jnp.where(lane128 == k, column, columns)
            values = jnp.transpose(columns)[0:8]
            if d == 0:
                vrecv[par, 0] = values
            else:
                vsend[d] = values
                v_copies[d] = remote(
                    vsend.at[d], vrecv.at[par, 4 - d], v_ss.at[d], v_rs.at[par, 4 - d], (r, home)
                )
                v_copies[d].start()

        pl.when(r > 0)(x_up.wait_recv)
        pl.when(r < n_res - 1)(x_dn.wait_recv)
        pl.when(g > 0)(y_up.wait_recv)
        pl.when(g < n_grp - 1)(y_dn.wait_recv)
        for x in range(2):
            side, face = (0, 1) if x == 0 else (1, 0)
            for i in range(3):
                part = trans[face, i, 0, x] * hx[par, side, 0]
                for j in range(1, 3):
                    part = part + trans[face, i, j, x] * hx[par, side, j]
                low_y = trans[3, i, 0, x, 0:8, :] * hy[par, 0, x : x + 1, :]
                high_y = trans[2, i, 0, x, 8:16, :] * hy[par, 1, x : x + 1, :]
                for j in range(1, 3):
                    at = slice(j * 2 + x, j * 2 + x + 1)
                    low_y = low_y + trans[3, i, j, x, 0:8, :] * hy[par, 0, at, :]
                    high_y = high_y + trans[2, i, j, x, 8:16, :] * hy[par, 1, at, :]
                low = fld[dst, i, x, 0:8, :] - part[0:8]
                fld[dst, i, x, 0:8, :] = low - jnp.where(row8 == 0, low_y, 0.0)
                high = fld[dst, i, x, 8:16, :] - part[8:16]
                fld[dst, i, x, 8:16, :] = high - jnp.where(row8 == 7, high_y, 0.0)

        for d in (1, 3, 2):
            remote(vsend.at[d], vrecv.at[par, d], v_ss.at[d], v_rs.at[par, d], (r, g)).wait_recv()
        back = vrecv[par].reshape(32, 256)
        for b in range(8):
            value = jnp.sum(jnp.where(iota32 == target[b], back, 0.0), axis=0, keepdims=True)
            for i in range(3):
                term = jnp.broadcast_to(w2c[b, i : i + 1, :] * value, (32, 256))
                top = term.astype(BF16)
                rest = (term - top.astype(F32)).astype(BF16)
                for zh in range(2):
                    at = zh * 96 + i * 32
                    xs[at : at + 32, b * 256 : (b + 1) * 256] = hot[b, zh] * top
                    xs[192 + at : 192 + at + 32, b * 256 : (b + 1) * 256] = hot[b, zh] * rest
        got = jnp.dot(xs[...], spread[...], preferred_element_type=F32)
        got = got[:192] + got[192:]
        for zh in range(2):
            for i in range(3):
                for x in range(2):
                    at = zh * 96 + i * 32 + x * 16
                    zs = slice(zh * 256, (zh + 1) * 256)
                    fld[dst, i, x, :, zs] = fld[dst, i, x, :, zs] - got[at : at + 16]

        pl.when(r < n_res - 1)(x_up.wait_send)
        pl.when(r > 0)(x_dn.wait_send)
        pl.when(g < n_grp - 1)(y_up.wait_send)
        pl.when(g > 0)(y_dn.wait_send)
        for d in (1, 2, 3):
            c_copies[d].wait_send()
            v_copies[d].wait_send()

    def fold(block):
        half = block[0:8] + block[8:16]
        return (half[:, 0:128] + half[:, 128:256]) + (half[:, 256:384] + half[:, 384:512])

    def sums_start(pairs, par):
        row = jnp.zeros((1, 128), F32)
        for k, (a, b) in enumerate(pairs):
            total = jnp.zeros((8, 128), F32)
            for i in range(3):
                for x in range(2):
                    total = total + fold(fld[a, i, x] * fld[b, i, x])
            one = jnp.sum(jnp.sum(total, axis=0, keepdims=True), axis=1, keepdims=True)
            row = jnp.where(lane == k, one, row)
        rsend[0] = row
        rrecv[par, me] = row

        def send(k, carry):
            remote(rsend, rrecv.at[par, pl.ds(me, 1)], r_ss, r_rs.at[par], peer(k)).start()
            return carry

        lax.fori_loop(1, n_dev, send, 0)

    def sums_wait(par):
        some = rrecv.at[par, pl.ds(0, n_dev - 1)]
        pltpu.make_async_copy(some, some, r_rs.at[par]).wait()
        pltpu.make_async_copy(some, some, r_ss).wait()
        row = jnp.sum(rrecv[par], axis=0)
        return [
            jnp.sum(jnp.where(lane == k, row, 0.0), axis=1, keepdims=True) for k in range(4)
        ]

    def keep(at, value):
        scal[at] = jnp.broadcast_to(value, (8, 128))

    def kept(at):
        return scal[at, 0:1, 0:1]

    def wide(value):
        return jnp.broadcast_to(value, (16, 512))

    RHO, ALPHA, OMEGA = 0, 1, 2

    def middle_step(par):
        inner, square, _, _ = sums_wait(par)
        omega = inner / square
        keep(OMEGA, omega)
        om, al = wide(omega), wide(kept(ALPHA))
        return om, al

    def step(j, carry):
        par = lax.rem(j, 2)
        odd = par == 1
        first = j == 0
        src = jnp.where(odd, W, jnp.where(first, R, Z))
        dst = jnp.where(odd, T, jnp.where(first, W, V))
        spmv(src, dst, par)

        @pl.when(jnp.logical_not(odd))
        def _():
            @pl.when(j > 0)
            def _():
                om, al = middle_step(1 - par)
                for i in range(3):
                    for x in range(2):
                        q, y = fld[Q, i, x], fld[Y, i, x]
                        fld[X, i, x] = fld[X, i, x] + al * fld[PP, i, x] + om * q
                        fld[R, i, x] = q - om * y
                        fld[W, i, x] = y - om * (fld[T, i, x] - al * fld[V, i, x])

            sums_start([(R0, R), (R0, W), (R0, S), (R0, Z)], par)

        @pl.when(odd)
        def _():
            rho_next, along_w, along_s, along_z = sums_wait(1 - par)
            omega = kept(OMEGA)
            beta = rho_next / kept(RHO) * (kept(ALPHA) / omega)
            beta = jnp.where(j == 1, 0.0, beta)
            alpha = rho_next / (along_w + beta * (along_s - omega * along_z))
            keep(RHO, rho_next)
            keep(ALPHA, alpha)
            be, om, al = wide(beta), wide(omega), wide(alpha)
            for i in range(3):
                for x in range(2):
                    s, z = fld[S, i, x], fld[Z, i, x]
                    res, w = fld[R, i, x], fld[W, i, x]
                    fld[PP, i, x] = res + be * (fld[PP, i, x] - om * s)
                    s = w + be * (s - om * z)
                    z = fld[T, i, x] + be * (z - om * fld[V, i, x])
                    fld[S, i, x] = s
                    fld[Z, i, x] = z
                    fld[Q, i, x] = res - al * s
                    fld[Y, i, x] = w - al * z
            sums_start([(Q, Y), (Y, Y)], par)

        return carry

    lax.fori_loop(0, 2 * ITERS, step, 0)
    om, al = middle_step(1)
    for i in range(3):
        for x in range(2):
            q = fld[Q, i, x]
            fld[X, i, x] = fld[X, i, x] + al * fld[PP, i, x] + om * q
            fld[R, i, x] = q - om * fld[Y, i, x]
    outs = [
        pltpu.make_async_copy(fld.at[X], x_out, out_sem.at[0]),
        pltpu.make_async_copy(fld.at[R], r_out, out_sem.at[1]),
    ]
    for copy in outs:
        copy.start()
    for copy in outs:
        copy.wait()


def solution(mesh):
    n_res, n_grp = mesh.shape["res"], mesh.shape["grp"]
    n_dev = n_res * n_grp

    def body(right_side, accumulation, transmissibility, completion, live_count, owner, c2w, w2c, inverse):
        dma = pltpu.SemaphoreType.DMA
        field = (3, 2, 16, 512)
        any_space = pl.BlockSpec(memory_space=pl.ANY)
        smem = pl.BlockSpec(memory_space=pltpu.SMEM)
        return pl.pallas_call(
            functools.partial(kernel, n_res, n_grp),
            name="bicgstab",
            out_shape=[jax.ShapeDtypeStruct(field, F32)] * 2,
            in_specs=[smem, smem] + [any_space] * 7,
            out_specs=[any_space] * 2,
            scratch_shapes=[
                pltpu.VMEM((11,) + field, F32),
                pltpu.VMEM((3, 3, 2, 16, 512), F32),
                pltpu.VMEM((6, 3, 3, 2, 16, 512), F32),
                pltpu.VMEM((4, 4, 256, 256), F32),
                pltpu.VMEM((8, 256), jnp.int32),
                pltpu.VMEM((8, 3, 256), F32),
                pltpu.VMEM((8, 3, 256), F32),
                pltpu.VMEM((8, 256, 256), BF16),
                pltpu.VMEM((2048, 256), BF16),
                pltpu.VMEM((8, 2, 32, 256), BF16),
                pltpu.VMEM((8, 192, 256), F32),
                pltpu.VMEM((384, 256), BF16),
                pltpu.VMEM((384, 2048), BF16),
                pltpu.VMEM((2, 2, 3, 16, 512), F32),
                pltpu.VMEM((2, 2, 8, 512), F32),
                pltpu.VMEM((2, 8, 512), F32),
                pltpu.VMEM((4, 8, 256), F32),
                pltpu.VMEM((2, 4, 8, 256), F32),
                pltpu.VMEM((4, 8, 256), F32),
                pltpu.VMEM((2, 4, 8, 256), F32),
                pltpu.VMEM((1, 1, 128), F32),
                pltpu.VMEM((2, n_dev, 1, 128), F32),
                pltpu.VMEM((4, 8, 128), F32),
                dma((15,)),
                dma((2,)),
                dma((2, 2)),
                dma((2,)),
                dma((2, 2)),
                dma((4,)),
                dma((2, 4)),
                dma((4,)),
                dma((2, 4)),
                dma(()),
                dma((2,)),
                dma((2,)),
            ],
            compiler_params=pltpu.CompilerParams(collective_id=0, has_side_effects=True),
        )(live_count, owner, right_side, accumulation, transmissibility, completion, c2w, w2c, inverse)

    in_specs = (
        P(None, "res", "grp", None),
        P(None, None, "res", "grp", None),
        P(None, None, None, "res", "grp", None),
        P(RES_GRP, None),
        P(RES_GRP),
        P(RES_GRP, None),
        P(RES_GRP, None, None),
        P(RES_GRP, None, None),
        P(RES_GRP, None, None, None, None),
    )
    out_specs = (P(None, "res", "grp", None), P(None, "res", "grp", None))

    def run(*args):
        first, second = jax.shard_map(
            body, mesh=mesh, in_specs=in_specs, out_specs=out_specs, check_vma=False
        )(*args)
        return first, second

    return run
```

time: 734 us -> 93.6 us (0.13)
  the two profiles are of different devices: /device:TPU:10 before, /device:TPU:1 now
where the time goes in v1:
time: 93.6 us; the launch traced here: 93.3 us
  Pallas kernels  85.3 us (91%)
  local copies, waits for them, and re-layouts  7.28 us (8%)
    pallas_call x1, Pallas kernels, body(): pl.pallas_call(functools.partial(kernel, n_res, n_grp), name='bicgstab',...  85.3 us
    unnamed x5, local copies, waits for them, and re-layouts  7.28 us

profile of v1, /device:TPU:1, one launch (start us, length us, event | category | flops | bytes accessed | tf_op | source)
XLA Modules:
  0.0 93.3 jit_solution(1238427561414370276)
XLA Ops:
  0.6 1.3 %copy.11.owner_ref = s32[8,1]{1,0:T(8,128)} copy(s32[8,1]{0,1:T(1,128)} %param.14) | data formatting | bytes 64 | tf_op args[5]
  1.9 1.4 %copy.12.c2w_hbm = f32[8,3,256]{2,1,0:T(4,128)} copy(f32[8,3,256]{2,0,1:T(8,128)} %param.15) | data formatting | bytes 49152 | tf_op args[6]
  3.3 1.4 %copy.13.w2c_hbm = f32[8,3,256]{2,1,0:T(4,128)} copy(f32[8,3,256]{2,0,1:T(8,128)} %param.16) | data formatting | bytes 49152 | tf_op args[7]
  4.7 85.3 %bicgstab.1 = (f32[3,2,16,512]{3,2,1,0:T(8,128)}, f32[3,2,16,512]{3,2,1,0:T(8,128)}) custom-call(s32[8]{0:T(128)} %live_ref.1, s32[8,1]{1,0:T(8,128)} %copy.11.owner_ref, f32[3,2,16,512]{3,2,1,0:T(8,128)} %rhs_hbm.1, f32[3,3,2,16,512]{4,3,2,1,0:T(8,128)} %acc_hbm.1, f32[6,3,3,2,16,512]{5,4,3,2,1,0:T(8,128)} %trans_hbm.1, s32[8,256]{1,0:T(8,128)} %comp_hbm.1, ...), custom_call_target="tpu_custom_call" | custom-call | tf_op jit(solution)/shard_map/bicgstab/pallas_call | solution.py:418
  90.0 1.6 %copy.16 = f32[3,2,16,512]{3,2,1,0:T(8,128)} copy(f32[3,2,16,512]{3,2,1,0:T(8,128)} %get-tuple-element.4) | data formatting | bytes 393216
  91.6 1.6 %copy.17 = f32[3,2,16,512]{3,2,1,0:T(8,128)} copy(f32[3,2,16,512]{3,2,1,0:T(8,128)} %get-tuple-element.5) | data formatting | bytes 393216

commit v2 on v1

v2 whole, which is shorter than its diff:
```python
import functools

import jax
import jax.numpy as jnp
from jax import lax
from jax.experimental import pallas as pl
from jax.experimental.pallas import tpu as pltpu
from jax.sharding import PartitionSpec as P

ITERS = 3
RES_GRP = ("res", "grp")
MESH, LOGICAL = pl.DeviceIdType.MESH, pl.DeviceIdType.LOGICAL
F32, BF16 = jnp.float32, jnp.bfloat16
R0, R, W, T, PP, S, Z, V, X, Q, Y, SPARE = range(12)


def kernel(
    n_res,
    n_grp,
    live_hbm,
    owner_hbm,
    rhs_hbm,
    acc_hbm,
    trans_hbm,
    comp_hbm,
    c2w_hbm,
    w2c_hbm,
    inv_hbm,
    x_out,
    r_out,
    live,
    owner,
    fld,
    diag,
    trans,
    inv,
    comp,
    c2w,
    w2c,
    picks,
    spread,
    hot,
    grid_of,
    lhs,
    xs,
    hx,
    hy,
    ysend,
    csend,
    crecv,
    vsend,
    vrecv,
    rsend,
    rrecv,
    scal,
    in_sem,
    hx_ss,
    hx_rs,
    hy_ss,
    hy_rs,
    c_ss,
    c_rs,
    v_ss,
    v_rs,
    r_ss,
    r_rs,
    out_sem,
):
    n_dev = n_res * n_grp
    r, g = lax.axis_index("res"), lax.axis_index("grp")
    me = r * n_grp + g

    def load(i, src, dst):
        return pltpu.make_async_copy(src, dst, in_sem.at[i])

    first_loads = [
        load(0, comp_hbm, comp),
        load(1, live_hbm, live),
        load(2, owner_hbm, owner),
        load(3, c2w_hbm, c2w),
        load(4, w2c_hbm, w2c),
        load(5, rhs_hbm, fld.at[R0]),
        load(6, rhs_hbm, fld.at[R]),
    ]
    face_loads = [load(7, acc_hbm, diag)] + [load(8 + f, trans_hbm.at[f], trans.at[f]) for f in range(6)]
    inverse_loads = [load(14 + h, inv_hbm.at[0, h], inv.at[h]) for h in range(4)]
    for copy in first_loads + face_loads + inverse_loads:
        copy.start()

    hx[...] = jnp.zeros_like(hx)
    hy[...] = jnp.zeros_like(hy)
    rrecv[...] = jnp.zeros_like(rrecv)

    barrier = pltpu.get_barrier_semaphore()

    def peer(k):
        return (me + k) & (n_dev - 1)

    def greet(k, carry):
        pl.semaphore_signal(barrier, inc=1, device_id=peer(k), device_id_type=LOGICAL)
        return carry

    lax.fori_loop(1, n_dev, greet, 0)

    for field in (T, PP, S, Z, V, X, Y):
        fld[field] = jnp.zeros((3, 2, 16, 512), F32)
    scal[...] = jnp.ones_like(scal)
    csend[...] = jnp.zeros_like(csend)
    ysend[...] = jnp.zeros_like(ysend)

    for copy in first_loads[:5]:
        copy.wait()
    owners = [owner[0, b] for b in range(8)]
    target = []
    for b in range(8):
        slot = jnp.int32(0)
        for a in range(b):
            slot = slot + jnp.where(owners[a] == owners[b], 1, 0).astype(jnp.int32)
        target.append(((owners[b] - g) & (n_grp - 1)) * 4 + slot)

    seg = lax.broadcasted_iota(jnp.int32, (8, 256), 1)
    well = lax.broadcasted_iota(jnp.int32, (8, 256), 0)
    lives = jnp.zeros((8, 256), jnp.int32)
    for b in range(8):
        lives = jnp.where(well == b, live[b], lives)
    for i in range(3):
        c2w[i] = jnp.where(seg < lives, c2w[i], 0.0)
        w2c[i] = jnp.where(seg < lives, w2c[i], 0.0)
    for b in range(8):
        cell = comp[b : b + 1, :]
        low = cell & 255
        half = (cell >> 8) & 1
        high = cell >> 9
        one = jnp.where(lax.broadcasted_iota(jnp.int32, (256, 256), 0) == low, 1.0, 0.0).astype(F32)
        picks[b] = one.astype(BF16)
        spread[b * 256 : (b + 1) * 256, :] = jnp.transpose(one).astype(BF16)
        rows = lax.broadcasted_iota(jnp.int32, (32, 256), 0)
        for zh in range(2):
            here = (rows == high) & (half == zh)
            hot[b, zh] = jnp.where(here, 1.0, 0.0).astype(BF16)
            for i in range(3):
                grid_of[b, zh * 96 + i * 32 : zh * 96 + (i + 1) * 32, :] = jnp.where(
                    here, c2w[i, b : b + 1, :], 0.0
                )
    for copy in first_loads[5:]:
        copy.wait()

    def remote(src, dst, ss, rs, device):
        return pltpu.make_async_remote_copy(
            src_ref=src, dst_ref=dst, send_sem=ss, recv_sem=rs, device_id=device, device_id_type=MESH
        )

    lane512 = lax.broadcasted_iota(jnp.int32, (8, 512), 1)
    row8 = lax.broadcasted_iota(jnp.int32, (8, 512), 0)
    iota4 = lax.broadcasted_iota(jnp.int32, (4, 256), 0)
    iota16 = lax.broadcasted_iota(jnp.int32, (16, 256), 0)
    lane = lax.broadcasted_iota(jnp.int32, (1, 128), 1)
    RHO, ALPHA, OMEGA, BETA = 0, 1, 2, 3

    def keep(at, value):
        scal[at] = jnp.broadcast_to(value, (8, 128))

    def kept(at):
        return scal[at, 0:1, 0:1]

    def wide(value):
        return jnp.broadcast_to(value, (16, 512))

    def fold(block):
        half = block[0:8] + block[8:16]
        return (half[:, 0:128] + half[:, 128:256]) + (half[:, 256:384] + half[:, 384:512])

    def sums_start(totals, par):
        row = jnp.zeros((1, 128), F32)
        for k, total in enumerate(totals):
            one = jnp.sum(jnp.sum(total, axis=0, keepdims=True), axis=1, keepdims=True)
            row = jnp.where(lane == k, one, row)
        rsend[0] = row
        rrecv[par, me] = row

        def send(k, carry):
            pltpu.make_async_remote_copy(
                src_ref=rsend,
                dst_ref=rrecv.at[par, pl.ds(me, 1)],
                send_sem=r_ss,
                recv_sem=r_rs.at[par],
                device_id=peer(k),
                device_id_type=LOGICAL,
            ).start()
            return carry

        lax.fori_loop(1, n_dev, send, 0)

    def sums_wait(par):
        some = rrecv.at[par, pl.ds(0, n_dev - 1)]
        pltpu.make_async_copy(some, some, r_rs.at[par]).wait()
        pltpu.make_async_copy(some, some, r_ss).wait()

    def sums_of(par):
        row = jnp.sum(rrecv[par], axis=0)
        return [jnp.sum(jnp.where(lane == k, row, 0.0), axis=1, keepdims=True) for k in range(4)]

    tiles = [(i, x) for i in range(3) for x in range(2)]

    def odd_rest(par):
        be, om, al = wide(kept(BETA)), wide(kept(OMEGA)), wide(kept(ALPHA))
        inner, square = jnp.zeros((8, 128), F32), jnp.zeros((8, 128), F32)
        for i, x in tiles:
            s, res, w = fld[S, i, x], fld[R, i, x], fld[W, i, x]
            fld[PP, i, x] = res + be * (fld[PP, i, x] - om * s)
            s = w + be * (s - om * fld[Q, i, x])
            fld[S, i, x] = s
            q = res - al * s
            y = w - al * fld[Z, i, x]
            fld[Q, i, x] = q
            fld[Y, i, x] = y
            inner = inner + fold(q * y)
            square = square + fold(y * y)
        sums_start([inner, square], par)

    def step(j, carry):
        par = j & 1
        odd = par == 1
        first = j == 0
        src = jnp.where(odd, W, jnp.where(first, R, Z))
        dst = jnp.where(odd, T, jnp.where(first, W, V))

        for zh in range(2):
            v = fld[src, :, :, :, zh * 256 : (zh + 1) * 256].reshape(96, 256)
            top = v.astype(BF16)
            lhs[zh * 96 : (zh + 1) * 96, :] = top
            lhs[192 + zh * 96 : 192 + (zh + 1) * 96, :] = (v - top.astype(F32)).astype(BF16)
        out = jnp.zeros((16, 256), F32)
        for b in range(8):
            got = jnp.dot(lhs[...], picks[b], preferred_element_type=F32)
            row = jnp.sum((got[:192] + got[192:]) * grid_of[b], axis=0, keepdims=True)
            out = jnp.where(iota16 == target[b], row, out)
        for d in range(4):
            csend[d] = out[d * 4 : (d + 1) * 4]
        for k in range(2):
            for x in range(2):
                for j3 in range(3):
                    at = j3 * 2 + x
                    edge = 15 if k == 0 else 0
                    ysend[k, at : at + 1, :] = fld[src, j3, x, edge : edge + 1, :]

        @pl.when(first)
        def _():
            pl.semaphore_wait(barrier, n_dev - 1)

        c_copies = {}
        for d in (2, 1, 3):
            to = (r, (g + d) & (n_grp - 1))
            c_copies[d] = remote(csend.at[d], crecv.at[par, 4 - d], c_ss.at[d], c_rs.at[par, 4 - d], to)
            c_copies[d].start()

        x_up = remote(fld.at[src, :, 1], hx.at[par, 0], hx_ss.at[0], hx_rs.at[par, 0], (r + 1, g))
        x_dn = remote(fld.at[src, :, 0], hx.at[par, 1], hx_ss.at[1], hx_rs.at[par, 1], (r - 1, g))
        y_up = remote(ysend.at[0], hy.at[par, 0], hy_ss.at[0], hy_rs.at[par, 0], (r, g + 1))
        y_dn = remote(ysend.at[1], hy.at[par, 1], hy_ss.at[1], hy_rs.at[par, 1], (r, g - 1))
        pl.when(r < n_res - 1)(x_up.start)
        pl.when(r > 0)(x_dn.start)
        pl.when(g < n_grp - 1)(y_up.start)
        pl.when(g > 0)(y_dn.start)

        @pl.when(odd)
        def _():
            @pl.when(j > 1)
            def _():
                om, al = wide(kept(OMEGA)), wide(kept(ALPHA))
                for i, x in tiles:
                    q = fld[Q, i, x]
                    fld[X, i, x] = fld[X, i, x] + al * fld[PP, i, x] + om * q
                    fld[R, i, x] = q - om * fld[Y, i, x]

            totals = [jnp.zeros((8, 128), F32)] * 4
            for i, x in tiles:
                shadow = fld[R0, i, x]
                for k, field in enumerate((R, W, S, Z)):
                    totals[k] = totals[k] + fold(shadow * fld[field, i, x])
            sums_start(totals, par)

        pl.when(jnp.logical_not(odd) & (j > 0))(lambda: odd_rest(par))

        @pl.when(first)
        def _():
            for copy in face_loads:
                copy.wait()
            for x in range(2):
                for i in range(3):
                    for k in range(3):
                        total = diag[i, k, x]
                        for f in range(6):
                            total = total + trans[f, i, k, x]
                        diag[i, k, x] = total
            for copy in inverse_loads:
                copy.wait()

        for x in range(2):
            for yt in range(2):
                ys = slice(yt * 8, yt * 8 + 8)
                sums = [None] * 3
                for k in range(3):
                    v = fld[src, k, x, ys, :]
                    zp = jnp.where(lane512 == 511, 0.0, pltpu.roll(v, 511, 1))
                    zm = jnp.where(lane512 == 0, 0.0, pltpu.roll(v, 1, 1))
                    if yt == 0:
                        yp = fld[src, k, x, 1:9, :]
                        ym = jnp.where(row8 == 0, 0.0, pltpu.roll(v, 1, 0))
                    else:
                        yp = jnp.where(row8 == 7, 0.0, pltpu.roll(v, 7, 0))
                        ym = fld[src, k, x, 7:15, :]
                    xn = fld[src, k, 1 - x, ys, :]
                    for i in range(3):
                        part = diag[i, k, x, ys, :] * v
                        part = part - trans[x, i, k, x, ys, :] * xn
                        part = part - trans[2, i, k, x, ys, :] * yp
                        part = part - trans[3, i, k, x, ys, :] * ym
                        part = part - trans[4, i, k, x, ys, :] * zp
                        part = part - trans[5, i, k, x, ys, :] * zm
                        sums[i] = part if sums[i] is None else sums[i] + part
                for i in range(3):
                    fld[dst, i, x, ys, :] = sums[i]

        lane128 = lax.broadcasted_iota(jnp.int32, (256, 128), 1)
        v_copies = {}
        for d in (0, 1, 3, 2):
            home = (g + d) & (n_grp - 1)
            if d == 0:
                c4 = csend[0]
            else:
                remote(csend.at[d], crecv.at[par, d], c_ss.at[d], c_rs.at[par, d], (r, home)).wait_recv()
                c4 = crecv[par, d]
            columns = jnp.zeros((256, 128), F32)
            for k in range(4):
                column = jnp.sum(inv[home, k] * c4[k : k + 1, :], axis=1, keepdims=True)
                columns = jnp.where(lane128 == k, column, columns)
            values = jnp.transpose(columns)[0:4]
            if d == 0:
                vrecv[par, 0] = values
            else:
                vsend[d] = values
                v_copies[d] = remote(
                    vsend.at[d], vrecv.at[par, 4 - d], v_ss.at[d], v_rs.at[par, 4 - d], (r, home)
                )
                v_copies[d].start()

        pl.when(r > 0)(x_up.wait_recv)
        pl.when(r < n_res - 1)(x_dn.wait_recv)
        pl.when(g > 0)(y_up.wait_recv)
        pl.when(g < n_grp - 1)(y_dn.wait_recv)
        for x in range(2):
            side, face = (0, 1) if x == 0 else (1, 0)
            for i in range(3):
                part = trans[face, i, 0, x] * hx[par, side, 0]
                for k in range(1, 3):
                    part = part + trans[face, i, k, x] * hx[par, side, k]
                low_y = trans[3, i, 0, x, 0:8, :] * hy[par, 0, x : x + 1, :]
                high_y = trans[2, i, 0, x, 8:16, :] * hy[par, 1, x : x + 1, :]
                for k in range(1, 3):
                    at = slice(k * 2 + x, k * 2 + x + 1)
                    low_y = low_y + trans[3, i, k, x, 0:8, :] * hy[par, 0, at, :]
                    high_y = high_y + trans[2, i, k, x, 8:16, :] * hy[par, 1, at, :]
                low = fld[dst, i, x, 0:8, :] - part[0:8]
                fld[dst, i, x, 0:8, :] = low - jnp.where(row8 == 0, low_y, 0.0)
                high = fld[dst, i, x, 8:16, :] - part[8:16]
                fld[dst, i, x, 8:16, :] = high - jnp.where(row8 == 7, high_y, 0.0)

        pl.when(r < n_res - 1)(x_up.wait_send)
        pl.when(r > 0)(x_dn.wait_send)
        pl.when(g < n_grp - 1)(y_up.wait_send)
        pl.when(g > 0)(y_dn.wait_send)
        for d in (1, 2, 3):
            c_copies[d].wait_send()
            v_copies[d].wait_send()

        pl.when(j > 0)(lambda: sums_wait(par))
        for d in (1, 3, 2):
            remote(vsend.at[d], vrecv.at[par, d], v_ss.at[d], v_rs.at[par, d], (r, g)).wait_recv()

        back = [vrecv[par, d] for d in range(4)]
        for b in range(8):
            part = jnp.zeros((4, 256), F32)
            for d in range(4):
                part = jnp.where(iota4 == target[b] - 4 * d, back[d], part)
            value = jnp.sum(part, axis=0, keepdims=True)
            for i in range(3):
                term = jnp.broadcast_to(w2c[i, b : b + 1, :] * value, (32, 256))
                top = term.astype(BF16)
                rest = (term - top.astype(F32)).astype(BF16)
                for zh in range(2):
                    at = zh * 96 + i * 32
                    xs[at : at + 32, b * 256 : (b + 1) * 256] = hot[b, zh] * top
                    xs[192 + at : 192 + at + 32, b * 256 : (b + 1) * 256] = hot[b, zh] * rest
        got = jnp.dot(xs[...], spread[...], preferred_element_type=F32)
        got = got[:192] + got[192:]

        d0, d1, d2, d3 = sums_of(par)
        rho, alpha, omega = kept(RHO), kept(ALPHA), kept(OMEGA)
        beta = jnp.where(j == 1, 0.0, d0 / rho * (alpha / omega))
        alpha_next = d0 / (d1 + beta * (d2 - omega * d3))
        omega_next = d0 / d1
        even = jnp.logical_not(odd) & (j > 0)
        keep(RHO, jnp.where(odd, d0, rho))
        keep(ALPHA, jnp.where(odd, alpha_next, alpha))
        keep(BETA, beta)
        keep(OMEGA, jnp.where(even, omega_next, omega))

        outer = wide(jnp.where(odd, beta, -omega_next))
        inner = wide(jnp.where(odd, omega, alpha))
        for zh in range(2):
            for i in range(3):
                for x in range(2):
                    at = zh * 96 + i * 32 + x * 16
                    zs = slice(zh * 256, (zh + 1) * 256)
                    fld[dst, i, x, :, zs] = fld[dst, i, x, :, zs] - got[at : at + 16]

        @pl.when(j > 0)
        def _():
            base = jnp.where(odd, T, Y)
            last = jnp.where(odd, Z, T)
            new = jnp.where(odd, Z, W)
            kept_in = jnp.where(odd, Q, SPARE)
            for i, x in tiles:
                old = fld[last, i, x]
                value = fld[base, i, x] + outer * (old - inner * fld[V, i, x])

                fld[kept_in, i, x] = old
                fld[new, i, x] = value

        return carry

    lax.fori_loop(0, 2 * ITERS, step, 0)
    odd_rest(0)
    sums_wait(0)
    inner, square, _, _ = sums_of(0)
    om, al = wide(inner / square), wide(kept(ALPHA))
    for i, x in tiles:
        q = fld[Q, i, x]
        fld[X, i, x] = fld[X, i, x] + al * fld[PP, i, x] + om * q
        fld[R, i, x] = q - om * fld[Y, i, x]
    outs = [
        pltpu.make_async_copy(fld.at[X], x_out, out_sem.at[0]),
        pltpu.make_async_copy(fld.at[R], r_out, out_sem.at[1]),
    ]
    for copy in outs:
        copy.start()
    for copy in outs:
        copy.wait()


def solution(mesh):
    n_res, n_grp = mesh.shape["res"], mesh.shape["grp"]
    n_dev = n_res * n_grp

    def body(right_side, accumulation, transmissibility, completion, live_count, owner, c2w, w2c, inverse):
        dma = pltpu.SemaphoreType.DMA
        field = (3, 2, 16, 512)
        any_space = pl.BlockSpec(memory_space=pl.ANY)
        return pl.pallas_call(
            functools.partial(kernel, n_res, n_grp),
            name="bicgstab",
            out_shape=[jax.ShapeDtypeStruct(field, F32)] * 2,
            in_specs=[any_space] * 9,
            out_specs=[any_space] * 2,
            scratch_shapes=[
                pltpu.SMEM((8,), jnp.int32),
                pltpu.SMEM((1, 8), jnp.int32),
                pltpu.VMEM((12,) + field, F32),
                pltpu.VMEM((3, 3, 2, 16, 512), F32),
                pltpu.VMEM((6, 3, 3, 2, 16, 512), F32),
                pltpu.VMEM((4, 4, 256, 256), F32),
                pltpu.VMEM((8, 256), jnp.int32),
                pltpu.VMEM((3, 8, 256), F32),
                pltpu.VMEM((3, 8, 256), F32),
                pltpu.VMEM((8, 256, 256), BF16),
                pltpu.VMEM((2048, 256), BF16),
                pltpu.VMEM((8, 2, 32, 256), BF16),
                pltpu.VMEM((8, 192, 256), F32),
                pltpu.VMEM((384, 256), BF16),
                pltpu.VMEM((384, 2048), BF16),
                pltpu.VMEM((2, 2, 3, 16, 512), F32),
                pltpu.VMEM((2, 2, 8, 512), F32),
                pltpu.VMEM((2, 8, 512), F32),
                pltpu.VMEM((4, 4, 256), F32),
                pltpu.VMEM((2, 4, 4, 256), F32),
                pltpu.VMEM((4, 4, 256), F32),
                pltpu.VMEM((2, 4, 4, 256), F32),
                pltpu.VMEM((1, 1, 128), F32),
                pltpu.VMEM((2, n_dev, 1, 128), F32),
                pltpu.VMEM((4, 8, 128), F32),
                dma((18,)),
                dma((2,)),
                dma((2, 2)),
                dma((2,)),
                dma((2, 2)),
                dma((4,)),
                dma((2, 4)),
                dma((4,)),
                dma((2, 4)),
                dma(()),
                dma((2,)),
                dma((2,)),
            ],
            compiler_params=pltpu.CompilerParams(collective_id=0, has_side_effects=True),
        )(
            live_count,
            owner.T,
            right_side,
            accumulation,
            transmissibility,
            completion,
            jnp.transpose(c2w, (1, 0, 2)),
            jnp.transpose(w2c, (1, 0, 2)),
            inverse,
        )

    in_specs = (
        P(None, "res", "grp", None),
        P(None, None, "res", "grp", None),
        P(None, None, None, "res", "grp", None),
        P(RES_GRP, None),
        P(RES_GRP),
        P(RES_GRP, None),
        P(RES_GRP, None, None),
        P(RES_GRP, None, None),
        P(RES_GRP, None, None, None, None),
    )
    out_specs = (P(None, "res", "grp", None), P(None, "res", "grp", None))

    def run(*args):
        first, second = jax.shard_map(
            body, mesh=mesh, in_specs=in_specs, out_specs=out_specs, check_vma=False
        )(*args)
        return first, second

    return run
```

time: 93.6 us -> 76.6 us (0.82)
  Pallas kernels: 85.3 us -> 72.6 us
  local copies, waits for them, and re-layouts: 7.28 us -> 3.23 us
    pallas_call x1, Pallas kernels: 85.3 us -> 72.6 us  [body(): pl.pallas_call(functools.partial(kernel, n_res, n_grp), name='bicgstab',...]
    unnamed x5 -> x2, local copies, waits for them, and re-layouts: 7.28 us -> 3.23 us
where the time goes in v2:
time: 76.6 us; the launch traced here: 76.5 us
  Pallas kernels  72.6 us (95%)
  local copies, waits for them, and re-layouts  3.23 us (4%)
    pallas_call x1, Pallas kernels, body(): pl.pallas_call(functools.partial(kernel, n_res, n_grp), name='bicgstab',...  72.6 us
    unnamed x2, local copies, waits for them, and re-layouts  3.23 us

profile of v2, /device:TPU:1, one launch (start us, length us, event | category | flops | bytes accessed | tf_op | source)
XLA Modules:
  0.0 76.5 jit_solution(6937605322167902479)
XLA Ops:
  0.6 72.6 %bicgstab.1 = (f32[3,2,16,512]{3,2,1,0:T(8,128)}, f32[3,2,16,512]{3,2,1,0:T(8,128)}) custom-call(s32[8]{0:T(128)} %live_hbm.1, s32[1,8]{1,0:T(1,128)} %bitcast.5, f32[3,2,16,512]{3,2,1,0:T(8,128)} %rhs_hbm.1, f32[3,3,2,16,512]{4,3,2,1,0:T(8,128)} %acc_hbm.1, f32[6,3,3,2,16,512]{5,4,3,2,1,0:T(8,128)} %trans_hbm.1, s32[8,256]{1,0:T(8,128)} %comp_hbm.1, ...), custom_call_target="tpu_custom_call" | custom-call | tf_op jit(solution)/shard_map/bicgstab/pallas_call | solution.py:460
  73.2 1.6 %copy.13 = f32[3,2,16,512]{3,2,1,0:T(8,128)} copy(f32[3,2,16,512]{3,2,1,0:T(8,128)} %get-tuple-element.4) | data formatting | bytes 393216
  74.8 1.6 %copy.14 = f32[3,2,16,512]{3,2,1,0:T(8,128)} copy(f32[3,2,16,512]{3,2,1,0:T(8,128)} %get-tuple-element.5) | data formatting | bytes 393216

commit v3 on v2

--- a/solution.py
+++ b/solution.py
@@ -8,10 +8,11 @@
 from jax.sharding import PartitionSpec as P
 
 ITERS = 3
+TOGETHER = 8
 RES_GRP = ("res", "grp")
 MESH, LOGICAL = pl.DeviceIdType.MESH, pl.DeviceIdType.LOGICAL
 F32, BF16 = jnp.float32, jnp.bfloat16
-R0, R, W, T, PP, S, Z, V, X, Q, Y, SPARE = range(12)
+R0, R, W, T, PP, S, Z, V, X, Q, Y = range(11)
 
 
 def kernel(
@@ -64,7 +65,6 @@
     v_rs,
     r_ss,
     r_rs,
-    out_sem,
 ):
     n_dev = n_res * n_grp
     r, g = lax.axis_index("res"), lax.axis_index("grp")
@@ -96,15 +96,23 @@
     def peer(k):
         return (me + k) & (n_dev - 1)
 
-    def greet(k, carry):
-        pl.semaphore_signal(barrier, inc=1, device_id=peer(k), device_id_type=LOGICAL)
-        return carry
-
-    lax.fori_loop(1, n_dev, greet, 0)
-
-    for field in (T, PP, S, Z, V, X, Y):
+    def every_peer(act):
+        trips, last = divmod(n_dev - 1, TOGETHER)
+
+        def trip(m, carry):
+            for u in range(TOGETHER):
+                act(1 + m * TOGETHER + u)
+            return carry
+
+        lax.fori_loop(0, trips, trip, 0)
+        for u in range(last):
+            act(1 + trips * TOGETHER + u)
+
+    every_peer(lambda k: pl.semaphore_signal(barrier, inc=1, device_id=peer(k), device_id_type=LOGICAL))
+
+    for field in (W, T, PP, S, Z, V, X, Q, Y):
         fld[field] = jnp.zeros((3, 2, 16, 512), F32)
-    scal[...] = jnp.ones_like(scal)
+    scal[...] = jnp.zeros_like(scal)
     csend[...] = jnp.zeros_like(csend)
     ysend[...] = jnp.zeros_like(ysend)
 
@@ -170,15 +178,18 @@
         half = block[0:8] + block[8:16]
         return (half[:, 0:128] + half[:, 128:256]) + (half[:, 256:384] + half[:, 384:512])
 
-    def sums_start(totals, par):
+    def row_of(totals):
         row = jnp.zeros((1, 128), F32)
         for k, total in enumerate(totals):
             one = jnp.sum(jnp.sum(total, axis=0, keepdims=True), axis=1, keepdims=True)
             row = jnp.where(lane == k, one, row)
+        return row
+
+    def sums_start(row, par):
         rsend[0] = row
         rrecv[par, me] = row
 
-        def send(k, carry):
+        def send(k):
             pltpu.make_async_remote_copy(
                 src_ref=rsend,
                 dst_ref=rrecv.at[par, pl.ds(me, 1)],
@@ -187,9 +198,8 @@
                 device_id=peer(k),
                 device_id_type=LOGICAL,
             ).start()
-            return carry
-
-        lax.fori_loop(1, n_dev, send, 0)
+
+        every_peer(send)
 
     def sums_wait(par):
         some = rrecv.at[par, pl.ds(0, n_dev - 1)]
@@ -202,7 +212,7 @@
 
     tiles = [(i, x) for i in range(3) for x in range(2)]
 
-    def odd_rest(par):
+    def odd_rest():
         be, om, al = wide(kept(BETA)), wide(kept(OMEGA)), wide(kept(ALPHA))
         inner, square = jnp.zeros((8, 128), F32), jnp.zeros((8, 128), F32)
         for i, x in tiles:
@@ -216,14 +226,28 @@
             fld[Y, i, x] = y
             inner = inner + fold(q * y)
             square = square + fold(y * y)
-        sums_start([inner, square], par)
-
-    def step(j, carry):
-        par = j & 1
-        odd = par == 1
-        first = j == 0
-        src = jnp.where(odd, W, jnp.where(first, R, Z))
-        dst = jnp.where(odd, T, jnp.where(first, W, V))
+        return row_of([inner, square])
+
+    def phase(it, odd):
+        par = int(odd)
+        first = it == 0
+        src = W if odd else jnp.where(first, R, Z)
+        dst = T if odd else jnp.where(first, W, V)
+
+        if odd:
+            om, al = wide(kept(OMEGA)), wide(kept(ALPHA))
+            totals = [jnp.zeros((8, 128), F32)] * 4
+            for i, x in tiles:
+                q = fld[Q, i, x]
+                fld[X, i, x] = fld[X, i, x] + al * fld[PP, i, x] + om * q
+                res = q - om * fld[Y, i, x]
+                fld[R, i, x] = res
+                shadow = fld[R0, i, x]
+                for k, value in enumerate((res, fld[W, i, x], fld[S, i, x], fld[Z, i, x])):
+                    totals[k] = totals[k] + fold(shadow * value)
+            parts = row_of(totals)
+        else:
+            parts = odd_rest()
 
         for zh in range(2):
             v = fld[src, :, :, :, zh * 256 : (zh + 1) * 256].reshape(96, 256)
@@ -244,9 +268,11 @@
                     edge = 15 if k == 0 else 0
                     ysend[k, at : at + 1, :] = fld[src, j3, x, edge : edge + 1, :]
 
-        @pl.when(first)
-        def _():
-            pl.semaphore_wait(barrier, n_dev - 1)
+        if not odd:
+
+            @pl.when(first)
+            def _():
+                pl.semaphore_wait(barrier, n_dev - 1)
 
         c_copies = {}
         for d in (2, 1, 3):
@@ -262,39 +288,26 @@
         pl.when(r > 0)(x_dn.start)
         pl.when(g < n_grp - 1)(y_up.start)
         pl.when(g > 0)(y_dn.start)
-
-        @pl.when(odd)
-        def _():
-            @pl.when(j > 1)
+        if odd:
+            sums_start(parts, par)
+        else:
+            pl.when(it > 0)(lambda: sums_start(parts, par))
+
+        if not odd:
+
+            @pl.when(first)
             def _():
-                om, al = wide(kept(OMEGA)), wide(kept(ALPHA))
-                for i, x in tiles:
-                    q = fld[Q, i, x]
-                    fld[X, i, x] = fld[X, i, x] + al * fld[PP, i, x] + om * q
-                    fld[R, i, x] = q - om * fld[Y, i, x]
-
-            totals = [jnp.zeros((8, 128), F32)] * 4
-            for i, x in tiles:
-                shadow = fld[R0, i, x]
-                for k, field in enumerate((R, W, S, Z)):
-                    totals[k] = totals[k] + fold(shadow * fld[field, i, x])
-            sums_start(totals, par)
-
-        pl.when(jnp.logical_not(odd) & (j > 0))(lambda: odd_rest(par))
-
-        @pl.when(first)
-        def _():
-            for copy in face_loads:
-                copy.wait()
-            for x in range(2):
-                for i in range(3):
-                    for k in range(3):
-                        total = diag[i, k, x]
-                        for f in range(6):
-                            total = total + trans[f, i, k, x]
-                        diag[i, k, x] = total
-            for copy in inverse_loads:
-                copy.wait()
+                for copy in face_loads:
+                    copy.wait()
+                for x in range(2):
+                    for i in range(3):
+                        for k in range(3):
+                            total = diag[i, k, x]
+                            for f in range(6):
+                                total = total + trans[f, i, k, x]
+                            diag[i, k, x] = total
+                for copy in inverse_loads:
+                    copy.wait()
 
         for x in range(2):
             for yt in range(2):
@@ -374,7 +387,24 @@
             c_copies[d].wait_send()
             v_copies[d].wait_send()
 
-        pl.when(j > 0)(lambda: sums_wait(par))
+        if odd:
+            sums_wait(par)
+        else:
+            pl.when(it > 0)(lambda: sums_wait(par))
+        d0, d1, d2, d3 = sums_of(par)
+        rho, alpha, omega = kept(RHO), kept(ALPHA), kept(OMEGA)
+        if odd:
+            beta = jnp.where(first, 0.0, d0 / rho * (alpha / omega))
+            alpha_next = d0 / (d1 + beta * (d2 - omega * d3))
+            keep(RHO, d0)
+            keep(ALPHA, alpha_next)
+            keep(BETA, beta)
+            outer, inner = wide(beta), wide(omega)
+        else:
+            omega_next = jnp.where(first, 0.0, d0 / d1)
+            keep(OMEGA, omega_next)
+            outer, inner = wide(-omega_next), wide(alpha)
+
         for d in (1, 3, 2):
             remote(vsend.at[d], vrecv.at[par, d], v_ss.at[d], v_rs.at[par, d], (r, g)).wait_recv()
 
@@ -395,19 +425,6 @@
         got = jnp.dot(xs[...], spread[...], preferred_element_type=F32)
         got = got[:192] + got[192:]
 
-        d0, d1, d2, d3 = sums_of(par)
-        rho, alpha, omega = kept(RHO), kept(ALPHA), kept(OMEGA)
-        beta = jnp.where(j == 1, 0.0, d0 / rho * (alpha / omega))
-        alpha_next = d0 / (d1 + beta * (d2 - omega * d3))
-        omega_next = d0 / d1
-        even = jnp.logical_not(odd) & (j > 0)
-        keep(RHO, jnp.where(odd, d0, rho))
-        keep(ALPHA, jnp.where(odd, alpha_next, alpha))
-        keep(BETA, beta)
-        keep(OMEGA, jnp.where(even, omega_next, omega))
-
-        outer = wide(jnp.where(odd, beta, -omega_next))
-        inner = wide(jnp.where(odd, omega, alpha))
         for zh in range(2):
             for i in range(3):
                 for x in range(2):
@@ -415,34 +432,36 @@
                     zs = slice(zh * 256, (zh + 1) * 256)
                     fld[dst, i, x, :, zs] = fld[dst, i, x, :, zs] - got[at : at + 16]
 
-        @pl.when(j > 0)
-        def _():
-            base = jnp.where(odd, T, Y)
-            last = jnp.where(odd, Z, T)
-            new = jnp.where(odd, Z, W)
-            kept_in = jnp.where(odd, Q, SPARE)
+        if odd:
             for i, x in tiles:
-                old = fld[last, i, x]
-                value = fld[base, i, x] + outer * (old - inner * fld[V, i, x])
-
-                fld[kept_in, i, x] = old
-                fld[new, i, x] = value
-
+                old = fld[Z, i, x]
+                fld[Q, i, x] = old
+                fld[Z, i, x] = fld[T, i, x] + outer * (old - inner * fld[V, i, x])
+        else:
+
+            @pl.when(it > 0)
+            def _():
+                for i, x in tiles:
+                    fld[W, i, x] = fld[Y, i, x] + outer * (fld[T, i, x] - inner * fld[V, i, x])
+
+    def step(it, carry):
+        phase(it, False)
+        phase(it, True)
         return carry
 
-    lax.fori_loop(0, 2 * ITERS, step, 0)
-    odd_rest(0)
+    lax.fori_loop(0, ITERS, step, 0)
+    sums_start(odd_rest(), 0)
     sums_wait(0)
     inner, square, _, _ = sums_of(0)
     om, al = wide(inner / square), wide(kept(ALPHA))
     for i, x in tiles:
         q = fld[Q, i, x]
-        fld[X, i, x] = fld[X, i, x] + al * fld[PP, i, x] + om * q
-        fld[R, i, x] = q - om * fld[Y, i, x]
-    outs = [
-        pltpu.make_async_copy(fld.at[X], x_out, out_sem.at[0]),
-        pltpu.make_async_copy(fld.at[R], r_out, out_sem.at[1]),
-    ]
+        x_out[i, x] = fld[X, i, x] + al * fld[PP, i, x] + om * q
+        r_out[i, x] = q - om * fld[Y, i, x]
+
+
+def hand_out(x_in, r_in, x_out, r_out, sem):
+    outs = [pltpu.make_async_copy(x_in, x_out, sem.at[0]), pltpu.make_async_copy(r_in, r_out, sem.at[1])]
     for copy in outs:
         copy.start()
     for copy in outs:
@@ -457,16 +476,29 @@
         dma = pltpu.SemaphoreType.DMA
         field = (3, 2, 16, 512)
         any_space = pl.BlockSpec(memory_space=pl.ANY)
-        return pl.pallas_call(
+        vmem = pl.BlockSpec(memory_space=pltpu.VMEM)
+        operands = (
+            live_count,
+            owner.T,
+            right_side,
+            accumulation,
+            transmissibility,
+            completion,
+            jnp.transpose(c2w, (1, 0, 2)),
+            jnp.transpose(w2c, (1, 0, 2)),
+            inverse,
+        )
+        operands = [pltpu.with_memory_space_constraint(a, pltpu.HBM) for a in operands]
+        held = pl.pallas_call(
             functools.partial(kernel, n_res, n_grp),
             name="bicgstab",
             out_shape=[jax.ShapeDtypeStruct(field, F32)] * 2,
             in_specs=[any_space] * 9,
-            out_specs=[any_space] * 2,
+            out_specs=[vmem] * 2,
             scratch_shapes=[
                 pltpu.SMEM((8,), jnp.int32),
                 pltpu.SMEM((1, 8), jnp.int32),
-                pltpu.VMEM((12,) + field, F32),
+                pltpu.VMEM((11,) + field, F32),
                 pltpu.VMEM((3, 3, 2, 16, 512), F32),
                 pltpu.VMEM((6, 3, 3, 2, 16, 512), F32),
                 pltpu.VMEM((4, 4, 256, 256), F32),
@@ -500,20 +532,20 @@
                 dma((2, 4)),
                 dma(()),
                 dma((2,)),
-                dma((2,)),
             ],
-            compiler_params=pltpu.CompilerParams(collective_id=0, has_side_effects=True),
-        )(
-            live_count,
-            owner.T,
-            right_side,
-            accumulation,
-            transmissibility,
-            completion,
-            jnp.transpose(c2w, (1, 0, 2)),
-            jnp.transpose(w2c, (1, 0, 2)),
-            inverse,
-        )
+            compiler_params=pltpu.CompilerParams(
+                collective_id=0, has_side_effects=True, vmem_limit_bytes=24 << 20
+            ),
+        )(*operands)
+        return pl.pallas_call(
+            hand_out,
+            name="hand_out",
+            out_shape=[jax.ShapeDtypeStruct(field, F32)] * 2,
+            in_specs=[vmem] * 2,
+            out_specs=[any_space] * 2,
+            scratch_shapes=[dma((2,))],
+            compiler_params=pltpu.CompilerParams(vmem_limit_bytes=1 << 20),
+        )(*held)
 
     in_specs = (
         P(None, "res", "grp", None),

time: 76.6 us -> 72.7 us (0.949)
  local copies, waits for them, and re-layouts: 3.23 us -> 0 us
    unnamed x2 -> x0, local copies, waits for them, and re-layouts: 3.23 us -> none
    pallas_call x1, Pallas kernels: 72.6 us -> 71.2 us  [body(): pl.pallas_call(functools.partial(kernel, n_res, n_grp), name='bicgstab',...]
where the time goes in v3:
time: 72.7 us; the launch traced here: 72.6 us
  Pallas kernels  71.9 us (99%)
    pallas_call x1, Pallas kernels, body(): pl.pallas_call(functools.partial(kernel, n_res, n_grp), name='bicgstab',...  71.2 us

profile of v3, /device:TPU:1, one launch (start us, length us, event | category | flops | bytes accessed | tf_op | source)
XLA Modules:
  0.0 72.6 jit_solution(9170719976189156989)
XLA Ops:
  0.6 71.2 %bicgstab.1 = (f32[3,2,16,512]{3,2,1,0:T(8,128)S(1)}, f32[3,2,16,512]{3,2,1,0:T(8,128)S(1)}) custom-call(s32[8]{0:T(128)} %live_hbm.1, s32[1,8]{1,0:T(1,128)} %bitcast.5, f32[3,2,16,512]{3,2,1,0:T(8,128)} %rhs_hbm.1, f32[3,3,2,16,512]{4,3,2,1,0:T(8,128)} %acc_hbm.1, f32[6,3,3,2,16,512]{5,4,3,2,1,0:T(8,128)} %trans_hbm.1, s32[8,256]{1,0:T(8,128)} %comp_hbm.1, ...), custom_call_target="tpu_custom_call" | custom-call | tf_op jit(solution)/shard_map/bicgstab/pallas_call | solution.py:492
  71.8 0.8 %hand_out.1 = (f32[3,2,16,512]{3,2,1,0:T(8,128)}, f32[3,2,16,512]{3,2,1,0:T(8,128)}) custom-call(f32[3,2,16,512]{3,2,1,0:T(8,128)S(1)} %get-tuple-element.4.x_in, f32[3,2,16,512]{3,2,1,0:T(8,128)S(1)} %get-tuple-element.5.r_in), custom_call_target="tpu_custom_call" | custom-call | tf_op jit(solution)/shard_map/hand_out/pallas_call | solution.py:540

commit v4 on v3

--- a/solution.py
+++ b/solution.py
@@ -51,6 +51,7 @@
     crecv,
     vsend,
     vrecv,
+    pair,
     rsend,
     rrecv,
     scal,
@@ -63,12 +64,13 @@
     c_rs,
     v_ss,
     v_rs,
+    p_ss,
+    p_rs,
     r_ss,
     r_rs,
 ):
     n_dev = n_res * n_grp
     r, g = lax.axis_index("res"), lax.axis_index("grp")
-    me = r * n_grp + g
 
     def load(i, src, dst):
         return pltpu.make_async_copy(src, dst, in_sem.at[i])
@@ -93,11 +95,19 @@
 
     barrier = pltpu.get_barrier_semaphore()
 
-    def peer(k):
-        return (me + k) & (n_dev - 1)
-
-    def every_peer(act):
-        trips, last = divmod(n_dev - 1, TOGETHER)
+    chips = n_dev // 2
+    core = r & 1
+    chip = (r >> 1) * n_grp + g
+    mate = (r + 1 - 2 * core, g)
+    beside = r - 1 + 2 * core
+    has_beside = (beside >= 0) & (beside < n_res)
+
+    def teammate(k):
+        other = (chip + k) & (chips - 1)
+        return ((other >> (n_grp.bit_length() - 1)) * 2 + core) * n_grp + (other & (n_grp - 1))
+
+    def every_teammate(act):
+        trips, last = divmod(chips - 1, TOGETHER)
 
         def trip(m, carry):
             for u in range(TOGETHER):
@@ -108,7 +118,14 @@
         for u in range(last):
             act(1 + trips * TOGETHER + u)
 
-    every_peer(lambda k: pl.semaphore_signal(barrier, inc=1, device_id=peer(k), device_id_type=LOGICAL))
+    every_teammate(
+        lambda k: pl.semaphore_signal(barrier, inc=1, device_id=teammate(k), device_id_type=LOGICAL)
+    )
+    pl.semaphore_signal(barrier, inc=1, device_id=mate, device_id_type=MESH)
+
+    @pl.when(has_beside)
+    def _():
+        pl.semaphore_signal(barrier, inc=1, device_id=(beside, g), device_id_type=MESH)
 
     for field in (W, T, PP, S, Z, V, X, Q, Y):
         fld[field] = jnp.zeros((3, 2, 16, 512), F32)
@@ -185,24 +202,33 @@
             row = jnp.where(lane == k, one, row)
         return row
 
+    def to_mate(par):
+        return remote(pair.at[0, par], pair.at[1, par], p_ss, p_rs.at[par], mate)
+
     def sums_start(row, par):
+        pair[0, par, 0] = row
+        to_mate(par).start()
+
+    def sums_on(par):
+        to_mate(par).wait()
+        row = pair[0, par, 0] + pair[1, par, 0]
         rsend[0] = row
-        rrecv[par, me] = row
+        rrecv[par, chip] = row
 
         def send(k):
             pltpu.make_async_remote_copy(
                 src_ref=rsend,
-                dst_ref=rrecv.at[par, pl.ds(me, 1)],
+                dst_ref=rrecv.at[par, pl.ds(chip, 1)],
                 send_sem=r_ss,
                 recv_sem=r_rs.at[par],
-                device_id=peer(k),
+                device_id=teammate(k),
                 device_id_type=LOGICAL,
             ).start()
 
-        every_peer(send)
+        every_teammate(send)
 
     def sums_wait(par):
-        some = rrecv.at[par, pl.ds(0, n_dev - 1)]
+        some = rrecv.at[par, pl.ds(0, chips - 1)]
         pltpu.make_async_copy(some, some, r_rs.at[par]).wait()
         pltpu.make_async_copy(some, some, r_ss).wait()
 
@@ -272,7 +298,7 @@
 
             @pl.when(first)
             def _():
-                pl.semaphore_wait(barrier, n_dev - 1)
+                pl.semaphore_wait(barrier, chips + jnp.where(has_beside, 1, 0).astype(jnp.int32))
 
         c_copies = {}
         for d in (2, 1, 3):
@@ -339,6 +365,11 @@
         v_copies = {}
         for d in (0, 1, 3, 2):
             home = (g + d) & (n_grp - 1)
+            if d == 1:
+                if odd:
+                    sums_on(par)
+                else:
+                    pl.when(it > 0)(lambda: sums_on(par))
             if d == 0:
                 c4 = csend[0]
             else:
@@ -387,6 +418,33 @@
             c_copies[d].wait_send()
             v_copies[d].wait_send()
 
+        for d in (1, 3, 2):
+            remote(vsend.at[d], vrecv.at[par, d], v_ss.at[d], v_rs.at[par, d], (r, g)).wait_recv()
+
+        back = [vrecv[par, d] for d in range(4)]
+        for b in range(8):
+            part = jnp.zeros((4, 256), F32)
+            for d in range(4):
+                part = jnp.where(iota4 == target[b] - 4 * d, back[d], part)
+            value = jnp.sum(part, axis=0, keepdims=True)
+            for i in range(3):
+                term = jnp.broadcast_to(w2c[i, b : b + 1, :] * value, (32, 256))
+                top = term.astype(BF16)
+                rest = (term - top.astype(F32)).astype(BF16)
+                for zh in range(2):
+                    at = zh * 96 + i * 32
+                    xs[at : at + 32, b * 256 : (b + 1) * 256] = hot[b, zh] * top
+                    xs[192 + at : 192 + at + 32, b * 256 : (b + 1) * 256] = hot[b, zh] * rest
+        got = jnp.dot(xs[...], spread[...], preferred_element_type=F32)
+        got = got[:192] + got[192:]
+
+        for zh in range(2):
+            for i in range(3):
+                for x in range(2):
+                    at = zh * 96 + i * 32 + x * 16
+                    zs = slice(zh * 256, (zh + 1) * 256)
+                    fld[dst, i, x, :, zs] = fld[dst, i, x, :, zs] - got[at : at + 16]
+
         if odd:
             sums_wait(par)
         else:
@@ -405,33 +463,6 @@
             keep(OMEGA, omega_next)
             outer, inner = wide(-omega_next), wide(alpha)
 
-        for d in (1, 3, 2):
-            remote(vsend.at[d], vrecv.at[par, d], v_ss.at[d], v_rs.at[par, d], (r, g)).wait_recv()
-
-        back = [vrecv[par, d] for d in range(4)]
-        for b in range(8):
-            part = jnp.zeros((4, 256), F32)
-            for d in range(4):
-                part = jnp.where(iota4 == target[b] - 4 * d, back[d], part)
-            value = jnp.sum(part, axis=0, keepdims=True)
-            for i in range(3):
-                term = jnp.broadcast_to(w2c[i, b : b + 1, :] * value, (32, 256))
-                top = term.astype(BF16)
-                rest = (term - top.astype(F32)).astype(BF16)
-                for zh in range(2):
-                    at = zh * 96 + i * 32
-                    xs[at : at + 32, b * 256 : (b + 1) * 256] = hot[b, zh] * top
-                    xs[192 + at : 192 + at + 32, b * 256 : (b + 1) * 256] = hot[b, zh] * rest
-        got = jnp.dot(xs[...], spread[...], preferred_element_type=F32)
-        got = got[:192] + got[192:]
-
-        for zh in range(2):
-            for i in range(3):
-                for x in range(2):
-                    at = zh * 96 + i * 32 + x * 16
-                    zs = slice(zh * 256, (zh + 1) * 256)
-                    fld[dst, i, x, :, zs] = fld[dst, i, x, :, zs] - got[at : at + 16]
-
         if odd:
             for i, x in tiles:
                 old = fld[Z, i, x]
@@ -451,6 +482,7 @@
 
     lax.fori_loop(0, ITERS, step, 0)
     sums_start(odd_rest(), 0)
+    sums_on(0)
     sums_wait(0)
     inner, square, _, _ = sums_of(0)
     om, al = wide(inner / square), wide(kept(ALPHA))
@@ -518,8 +550,9 @@
                 pltpu.VMEM((2, 4, 4, 256), F32),
                 pltpu.VMEM((4, 4, 256), F32),
                 pltpu.VMEM((2, 4, 4, 256), F32),
+                pltpu.VMEM((2, 2, 1, 1, 128), F32),
                 pltpu.VMEM((1, 1, 128), F32),
-                pltpu.VMEM((2, n_dev, 1, 128), F32),
+                pltpu.VMEM((2, n_dev // 2, 1, 128), F32),
                 pltpu.VMEM((4, 8, 128), F32),
                 dma((18,)),
                 dma((2,)),
@@ -530,6 +563,8 @@
                 dma((2, 4)),
                 dma((4,)),
                 dma((2, 4)),
+                dma(()),
+                dma((2,)),
                 dma(()),
                 dma((2,)),
             ],

time: 72.7 us -> 72 us (level)
  no operation moved by 1% of the time
where the time goes in v4:
time: 72 us; the launch traced here: 71.9 us
  Pallas kernels  71.3 us (99%)
    pallas_call x1, Pallas kernels, body(): pl.pallas_call(functools.partial(kernel, n_res, n_grp), name='bicgstab',...  70.5 us

profile of v4, /device:TPU:1, one launch (start us, length us, event | category | flops | bytes accessed | tf_op | source)
XLA Modules:
  0.0 71.9 jit_solution(11237285304020464571)
XLA Ops:
  0.6 70.5 %bicgstab.1 = (f32[3,2,16,512]{3,2,1,0:T(8,128)S(1)}, f32[3,2,16,512]{3,2,1,0:T(8,128)S(1)}) custom-call(s32[8]{0:T(128)} %live_hbm.1, s32[1,8]{1,0:T(1,128)} %bitcast.5, f32[3,2,16,512]{3,2,1,0:T(8,128)} %rhs_hbm.1, f32[3,3,2,16,512]{4,3,2,1,0:T(8,128)} %acc_hbm.1, f32[6,3,3,2,16,512]{5,4,3,2,1,0:T(8,128)} %trans_hbm.1, s32[8,256]{1,0:T(8,128)} %comp_hbm.1, ...), custom_call_target="tpu_custom_call" | custom-call | tf_op jit(solution)/shard_map/bicgstab/pallas_call | solution.py:524
  71.2 0.8 %hand_out.1 = (f32[3,2,16,512]{3,2,1,0:T(8,128)}, f32[3,2,16,512]{3,2,1,0:T(8,128)}) custom-call(f32[3,2,16,512]{3,2,1,0:T(8,128)S(1)} %get-tuple-element.4.x_in, f32[3,2,16,512]{3,2,1,0:T(8,128)S(1)} %get-tuple-element.5.r_in), custom_call_target="tpu_custom_call" | custom-call | tf_op jit(solution)/shard_map/hand_out/pallas_call | solution.py:575
